TPU v7x, 256 devices: a whole 4x4x8 slice. The times are simulated.
256 devices in a mesh: dp: 64 (over x, z, core), mp: 4 (over y).
Axes of the slice: x: 4, y: 4, z: 8, core: 2. Of those that a mesh axis runs over, the one named last changes fastest.
Arguments:
- queries: bfloat16 [128, 16, 5120], P('dp', None, 'mp')
- key_value_cache: bfloat16 [3072, 2, 128, 1024], P('dp', None, None, 'mp'), may hold values from -6 to 6
- slot_tags: int32 [3072], P('dp'), may hold values from 0 to 127, as said below
- span_key_value: bfloat16 [128, 2, 16, 1024], P('dp', None, None, 'mp'), may hold values from -6 to 6
- answer_id: int32 [128], P('dp'), may hold values from 0 to 127
- w_cand: bfloat16 [5120, 128], P('mp')
Outputs:
- attended: bfloat16 [128, 16, 5120], P('dp', None, 'mp')
- chain_score: float32 [128], P('dp')
- answer_tally: float32 [8, 128], P(None, 'dp')
Inputs may be any that keep to these rules, and one draw needn't show every extreme that they name: `slot_tags`: among the 48 blocks of any one index of dp, at most 2 belong to the chains o * 2 to o * 2 + 1 of any one o, and for some o every index of dp holds exactly 2 such blocks. A chain may have no cached block.
All inputs are finite; a program needn't handle non-finite values.
Results may differ from a plain program's by a relative error of at most 0.0075.
Values may be sent and summed in bfloat16 or wider, within the bound.
A program may use at most 128 MiB of HBM per device.

v0:
```python
import jax
import jax.numpy as jnp
from jax import lax
from jax.sharding import PartitionSpec as P

QUERY_HEADS = 40
KEY_VALUE_HEADS = 8
HEAD_SIZE = 128
NCAND = 128
SAMPLES = 16


big_neg = -1e30


def from_everyone(x, axis):
    count = lax.axis_size(axis)
    return lax.all_to_all(jnp.broadcast_to(x[None], (count, *x.shape)), axis, 0, 0, tiled=True)


def taken_together(x, axis):
    everything = from_everyone(x, axis)
    return jnp.sum(everything, axis=0)


def split_up(x, dim, count):
    lengths = x.shape
    pieces = x.reshape(*lengths[:dim], count, lengths[dim] // count, *lengths[dim + 1 :])
    return jnp.moveaxis(pieces, dim, 0)


def sent_and_summed(x, axis, dim):
    count = lax.axis_size(axis)
    pieces = lax.all_to_all(split_up(x, dim, count), axis, 0, 0, tiled=True)
    return jnp.sum(pieces, axis=0)


def block_terms(picked, blocks, causal):
    count = picked.shape[0]
    span = picked.shape[1]
    width = blocks.shape[2]
    heads_kv = blocks.shape[3] // HEAD_SIZE
    head_group = QUERY_HEADS // KEY_VALUE_HEADS
    query_rows = picked.reshape(count, span, heads_kv, head_group, HEAD_SIZE)
    lookup_matrix = blocks[:, 0].reshape(count, width, heads_kv, HEAD_SIZE)
    value_rows = blocks[:, 1].reshape(count, width, heads_kv, HEAD_SIZE)
    logit_rows = jnp.einsum(
        "nakgd,nbkd->nkgab", query_rows, lookup_matrix, preferred_element_type=jnp.float32
    ) * HEAD_SIZE ** (-0.5)
    if causal:
        allowed = jnp.arange(span)[:, None] >= jnp.arange(width)[None, :]
        logit_rows = jnp.where(allowed, logit_rows, big_neg)
    peaks = jnp.max(logit_rows, axis=-1)
    weights = jnp.exp(logit_rows - peaks[..., None])
    totals = jnp.sum(weights, axis=-1)
    summed_scores = jnp.einsum(
        "nkgab,nbkd->nkgad",
        weights.astype(jnp.bfloat16),
        value_rows,
        preferred_element_type=jnp.float32,
    )
    return (peaks, totals, summed_scores)


def merge_items(peaks, totals, summed_scores, member):
    member_f = member.astype(jnp.float32)
    masked = jnp.where(member[:, :, None, None, None], peaks[:, None], big_neg)
    chain_peak = jnp.max(masked, axis=0)
    item_peak = jnp.einsum("nc,ckga->nkga", member_f, chain_peak, precision=lax.Precision.HIGHEST)
    present = jnp.any(member, axis=1)
    factor = jnp.where(present[:, None, None, None], jnp.exp(peaks - item_peak), 0.0)
    chain_total = jnp.einsum(
        "nc,nkga->ckga", member_f, totals * factor, precision=lax.Precision.HIGHEST
    )
    chain_sum = jnp.einsum(
        "nc,nkgad->ckgad",
        member_f,
        summed_scores * factor[..., None],
        precision=lax.Precision.HIGHEST,
    )
    return (chain_peak, chain_total, chain_sum)


def fold_sources(peaks, totals, summed_scores):
    overall = jnp.max(peaks, axis=0)
    factor = jnp.exp(peaks - overall[None])
    return (
        overall,
        jnp.sum(totals * factor, axis=0),
        jnp.sum(summed_scores * factor[..., None], axis=0),
    )


def fold_pair(first, second):
    overall = jnp.maximum(first[0], second[0])
    left = jnp.exp(first[0] - overall)
    right = jnp.exp(second[0] - overall)
    total = first[1] * left + second[1] * right
    summed_scores = first[2] * left[..., None] + second[2] * right[..., None]
    return (overall, total, summed_scores)


def per_device(queries, key_value_cache, slot_tags, span_key_value, answer_id, w_cand):
    accelerator_roster = lax.axis_size("dp")
    position = lax.axis_index("dp")
    chains_here = queries.shape[0]
    features = queries.shape[2]
    all_queries = lax.all_gather(queries, "dp", axis=0, tiled=True)
    picked = all_queries[slot_tags]
    peaks, totals, summed_scores = block_terms(picked, key_value_cache, False)
    member = (
        slot_tags[:, None] == jnp.arange(accelerator_roster * chains_here, dtype=jnp.int32)[None, :]
    )
    chain_peak, chain_total, chain_sum = merge_items(peaks, totals, summed_scores, member)
    grid = (accelerator_roster, chains_here)
    sent = (
        chain_sum.reshape(grid + chain_sum.shape[1:]),
        chain_total.reshape(grid + chain_total.shape[1:]),
        chain_peak.reshape(grid + chain_peak.shape[1:]),
    )
    got_sum, got_total, got_peak = (
        lax.all_to_all(sent[0], "dp", split_axis=0, concat_axis=0, tiled=True),
        lax.all_to_all(sent[1], "dp", split_axis=0, concat_axis=0, tiled=True),
        lax.all_to_all(sent[2], "dp", split_axis=0, concat_axis=0, tiled=True),
    )
    remote = fold_sources(got_peak, got_total, got_sum)
    own_span = block_terms(queries, span_key_value, True)
    final_peak, final_total, final_sum = fold_pair(own_span, remote)
    output = final_sum / final_total[..., None]
    output = jnp.transpose(output, (0, 3, 1, 2, 4)).reshape(chains_here, queries.shape[1], features)
    attended = output.astype(jnp.bfloat16)
    span = queries.shape[1]
    partial_logits = jnp.dot(
        attended.reshape(chains_here * span, features), w_cand, preferred_element_type=jnp.float32
    )
    logit_rows = taken_together(partial_logits, "mp").reshape(chains_here, span, NCAND)
    top_logit = jnp.max(logit_rows, axis=-1, keepdims=True)
    log_norm = top_logit[..., 0] + jnp.log(jnp.sum(jnp.exp(logit_rows - top_logit), axis=-1))
    answer_hot = (answer_id[:, None] == jnp.arange(NCAND, dtype=jnp.int32)[None, :]).astype(
        jnp.float32
    )
    chosen_logit = jnp.sum(logit_rows * answer_hot[:, None, :], axis=-1)
    chain_score = jnp.mean(chosen_logit - log_norm, axis=-1)
    prompt_count = accelerator_roster * chains_here // SAMPLES
    global_chain = position * chains_here + jnp.arange(chains_here, dtype=jnp.int32)
    prompt_hot = (
        (global_chain // SAMPLES)[:, None] == jnp.arange(prompt_count, dtype=jnp.int32)[None, :]
    ).astype(jnp.float32)
    tally_terms = jnp.dot(
        prompt_hot.T, chain_score[:, None] * answer_hot, precision=lax.Precision.HIGHEST
    )
    answer_tally = sent_and_summed(tally_terms, "dp", 1)
    return (attended, chain_score, answer_tally)


def solution(mesh):
    in_specs = (
        P("dp", None, "mp"),
        P("dp", None, None, "mp"),
        P("dp"),
        P("dp", None, None, "mp"),
        P("dp"),
        P("mp", None),
    )
    out_specs = (P("dp", None, "mp"), P("dp"), P(None, "dp"))
    return jax.shard_map(
        per_device, mesh=mesh, in_specs=in_specs, out_specs=out_specs, check_vma=False
    )
```

profile of v0, /device:TPU:1, one launch (start us, length us, event | category | flops | bytes accessed | tf_op | source)
XLA Modules:
  0.0 450.8 jit_solution(15284297287639628060)
XLA Ops:
  7.2 0.7 all-gather.2.cloned.1.call-update
  7.9 5.2 %fusion.48 = (bf16[48,1,128,256]{3,2,1,0:T(8,128)(2,1)}, bf16[48,1,128,256]{3,2,1,0:T(8,128)(2,1)S(1)}) fusion(bf16[48,2,128,256]{3,2,1,0:T(8,128)(2,1)} %param.7), kind=kLoop, calls=%fused_computation.74 | loop fusion | bytes 12582912 | tf_op jit(solution)/shard_map/slice | solution.py:45
  13.1 2.9 copy.195
  16.0 3.5 copy.194
  19.7 74.8 %all-gather.2.cloned.1.call-done = bf16[128,16,1280]{2,1,0:T(8,128)(2,1)} async-done(((bf16[2,16,1280]{2,1,0:T(8,128)(2,1)}), bf16[128,16,1280]{2,1,0:T(8,128)(2,1)}) %all-gather.2.cloned.1.call-update) | async-done | bytes 5242896 | tf_op jit(solution)/shard_map/all_gather | solution.py:108
  94.6 4.5 %gather_fusion = bf16[48,16,1280]{2,1,0:T(8,128)(2,1)} fusion(bf16[128,16,1280]{2,1,0:T(8,128)(2,1)} %all-gather.2.cloned.1.call-done, s32[1024]{0:T(1024)S(1)} %pad_clamp_fusion), kind=kCustom, calls=%fused_computation | custom fusion | bytes 3932352 | tf_op jit(solution)/shard_map/gather | solution.py:109
  99.1 5.6 %reshape.142 = bf16[48,16,2,5,128]{4,3,2,1,0:T(8,128)(2,1)} reshape(bf16[48,16,1280]{2,1,0:T(8,128)(2,1)} %gather_fusion) | data formatting | bytes 3932160 | tf_op jit(solution)/shard_map/reshape | solution.py:44
  104.7 5.7 %bitcast_reduce_fusion = (f32[48,2,5,16]{3,2,1,0:T(8,128)}, f32[48,2,16,5,128]{4,2,3,1,0:T(8,128)}) fusion(bf16[48,128,2,128,1]{1,3,4,2,0:T(8,128)(2,1)S(1)} %bitcast.94, bf16[48,16,2,5,128]{4,3,2,1,0:T(8,128)(2,1)} %reshape.142), kind=kOutput, calls=%fused_computation.3 | convolution fusion | flops 253616640 | bytes 9074688 | tf_op jit(solution)/shard_map/nakgd,nbkd->nkgab/dot_general | solution.py:47
  110.4 1.2 copy.158
  111.7 3.8 fusion.3
  115.6 1.2 select_reduce_fusion
  118.1 1.3 reshape.167
  119.5 6.0 %all-to-all-start.2 = ((f32[64,1,320]{2,1,0:T(1,128)}), f32[64,1,320]{2,1,0:T(1,128)S(1)}, u32[]{:S(2)}, u32[]{:S(2)}) async-start(f32[64,1,320]{2,1,0:T(1,128)} %reshape.167), calls=%async_computation.2 | async-start | bytes 196608 | tf_op jit(solution)/shard_map/all_to_all | solution.py:123
  125.5 5.8 %convolution_multiply_fusion = f32[48,2,5,16,128]{4,3,2,1,0:T(8,128)} fusion(bf16[48,128,2,128,1]{1,3,4,2,0:T(8,128)(2,1)} %bitcast.96, f32[48,2,16,5,128]{4,2,3,1,0:T(8,128)} %get-tuple-element.17, f32[48,2,5,16]{3,2,1,0:T(8,128)S(1)} %copy.159, f32[48,2,5,16]{3,2,1,0:T(8,128)S(1)} %copy-done.1), kind=kOutput, calls=%fused_computation.10 | convolution fusion | flops 255590400 | bytes 11071488 | tf_op jit(solution)/shard_map/nkgab,nbkd->nkgad/dot_general | solution.py:56
  131.8 1.3 reshape.165
  133.1 2.5 all-to-all-done.2
  135.6 7.9 %all-to-all-start = ((f32[64,1,320]{2,1,0:T(1,128)}), f32[64,1,320]{2,1,0:T(1,128)S(1)}, u32[]{:S(2)}, u32[]{:S(2)}) async-start(f32[64,1,320]{2,1,0:T(1,128)} %reshape.165), calls=%async_computation | async-start | bytes 196608 | tf_op jit(solution)/shard_map/all_to_all | solution.py:124
  143.5 8.7 %fusion.1 = f32[128,2,5,16,128]{4,0,3,2,1:T(8,128)S(1)} fusion(f32[48,2,5,16,128]{4,3,2,1,0:T(8,128)} %convolution_multiply_fusion, s32[48]{0:T(128)S(1)} %copy-done.4), kind=kOutput, calls=%fused_computation.5 | convolution fusion | flops 1509955584 | bytes 14418112 | tf_op jit(solution)/shard_map/nc,nkgad->ckgad/dot_general | solution.py:75
  152.2 7.1 %copy.161 = f32[64,2,2,5,16,128]{5,1,4,3,2,0:T(2,128)} copy(f32[64,2,2,5,16,128]{5,1,0,4,3,2:T(2,128)S(1)} %bitcast.93) | data formatting | bytes 20971520 | tf_op jit(solution)/shard_map/reshape | solution.py:117
  159.3 10.6 %all-to-all-start.1 = ((f32[64,2,2,5,16,128]{5,1,4,3,2,0:T(2,128)}), f32[64,2,2,5,16,128]{5,1,4,3,2,0:T(2,128)}, u32[]{:S(2)}, u32[]{:S(2)}) async-start(f32[64,2,2,5,16,128]{5,1,4,3,2,0:T(2,128)} %copy.161), calls=%async_computation.1 | async-start | bytes 20971520 | tf_op jit(solution)/shard_map/all_to_all | solution.py:122
  171.1 0.9 reduce.6
  172.8 0.9 reduce.7
  175.0 3.6 copy.164
  178.6 222.1 %all-to-all-done.1 = f32[64,2,2,5,16,128]{5,1,4,3,2,0:T(2,128)} async-done(((f32[64,2,2,5,16,128]{5,1,4,3,2,0:T(2,128)}), f32[64,2,2,5,16,128]{5,1,4,3,2,0:T(2,128)}, u32[]{:S(2)}, u32[]{:S(2)}) %all-to-all-start.1) | async-done | bytes 10485792 | tf_op jit(solution)/shard_map/all_to_all | solution.py:122
  400.7 14.3 %multiply_reduce_fusion = f32[2,2,5,16,128]{4,0,3,2,1:T(2,128)S(1)} fusion(f32[64,2,2,5,16,128]{5,1,4,3,2,0:T(2,128)} %all-to-all-done.1, f32[64,2,2,5,16]{1,4,3,2,0:T(8,128)} %copy.164), kind=kLoop, calls=%fused_computation.1 | loop fusion | flops 5201920 | bytes 10731520 | tf_op jit(solution)/shard_map/reduce_sum | solution.py:90
  415.6 0.6 broadcast_in_dim.52
  416.2 4.0 all-to-all-start.3
  420.2 5.0 %all-to-all-done.3 = f32[4,32,128]{2,1,0:T(8,128)S(1)} async-done(((f32[4,32,128]{2,1,0:T(8,128)}), f32[4,32,128]{2,1,0:T(8,128)S(1)}, u32[]{:S(2)}, u32[]{:S(2)}) %all-to-all-start.3) | async-done | bytes 65568 | tf_op jit(solution)/shard_map/all_to_all | solution.py:18
  425.9 1.0 fusion.34
  426.8 6.7 %all-to-all-start.4 = ((f32[64,8,2]{1,2,0:T(2,128)}), f32[64,8,2]{1,2,0:T(2,128)S(1)}, u32[]{:S(2)}, u32[]{:S(2)}) async-start(f32[64,8,2]{1,2,0:T(2,128)} %bitcast.25), calls=%async_computation.4 | async-start | bytes 131072 | tf_op jit(solution)/shard_map/all_to_all | solution.py:34
  433.6 0.7 convert_element_type.28
  434.3 9.0 %all-to-all-done.4 = f32[64,8,2]{1,2,0:T(2,128)S(1)} async-done(((f32[64,8,2]{1,2,0:T(2,128)}), f32[64,8,2]{1,2,0:T(2,128)S(1)}, u32[]{:S(2)}, u32[]{:S(2)}) %all-to-all-start.4) | async-done | bytes 4128 | tf_op jit(solution)/shard_map/all_to_all | solution.py:34
  (59 shorter events, 7.0 us)
Async XLA Ops:
  7.2 408.2 %copy-start = (bf16[1280,128]{1,0:T(8,128)(2,1)S(1)}, bf16[1280,128]{1,0:T(8,128)(2,1)}, u32[]{:S(2)}) copy-start(bf16[1280,128]{1,0:T(8,128)(2,1)} %param.11) | copy-start | bytes 983044
  7.2 87.4 %all-gather.2.cloned.1.call-start = ((), (), s32[]{:S(2)}) async-start(), calls=%async_computation.5 | async-start | bytes 5324800 | tf_op jit(solution)/shard_map/all_gather | solution.py:108
  16.0 3.5 copy-start.4
  110.4 5.2 %copy-start.1 = (f32[48,2,5,16]{3,2,1,0:T(8,128)S(1)}, f32[48,2,5,16]{3,2,1,0:T(8,128)}, u32[]{:S(2)}) copy-start(f32[48,2,5,16]{3,2,1,0:T(8,128)} %get-tuple-element.16) | copy-start | bytes 92164
  119.5 16.1 %all-to-all-start.2 = ((f32[64,1,320]{2,1,0:T(1,128)}), f32[64,1,320]{2,1,0:T(1,128)S(1)}, u32[]{:S(2)}, u32[]{:S(2)}) async-start(f32[64,1,320]{2,1,0:T(1,128)} %reshape.167), calls=%async_computation.2 | async-start | bytes 196608 | tf_op jit(solution)/shard_map/all_to_all | solution.py:123
  135.6 23.7 %all-to-all-start = ((f32[64,1,320]{2,1,0:T(1,128)}), f32[64,1,320]{2,1,0:T(1,128)S(1)}, u32[]{:S(2)}, u32[]{:S(2)}) async-start(f32[64,1,320]{2,1,0:T(1,128)} %reshape.165), calls=%async_computation | async-start | bytes 196608 | tf_op jit(solution)/shard_map/all_to_all | solution.py:124
  159.3 10.7 %copy-start.2 = (bf16[2,16,1280]{2,1,0:T(8,128)(2,1)S(1)}, bf16[2,16,1280]{2,1,0:T(8,128)(2,1)}, u32[]{:S(2)}) copy-start(bf16[2,16,1280]{2,1,0:T(8,128)(2,1)} %param.6) | copy-start | bytes 245764
  159.3 10.8 %copy-start.3 = (bf16[2,2,16,256]{3,2,1,0:T(8,128)(2,1)S(1)}, bf16[2,2,16,256]{3,2,1,0:T(8,128)(2,1)}, u32[]{:S(2)}) copy-start(bf16[2,2,16,256]{3,2,1,0:T(8,128)(2,1)} %param.9) | copy-start | bytes 98308
  159.3 11.2 %copy-start.5 = (s32[2]{0:T(128)S(1)}, s32[2]{0:T(128)}, u32[]{:S(2)}) copy-start(s32[2]{0:T(128)} %param.10) | copy-start | bytes 28
  159.3 241.3 %all-to-all-start.1 = ((f32[64,2,2,5,16,128]{5,1,4,3,2,0:T(2,128)}), f32[64,2,2,5,16,128]{5,1,4,3,2,0:T(2,128)}, u32[]{:S(2)}, u32[]{:S(2)}) async-start(f32[64,2,2,5,16,128]{5,1,4,3,2,0:T(2,128)} %copy.161), calls=%async_computation.1 | async-start | bytes 20971520 | tf_op jit(solution)/shard_map/all_to_all | solution.py:122
  416.2 9.0 %all-to-all-start.3 = ((f32[4,32,128]{2,1,0:T(8,128)}), f32[4,32,128]{2,1,0:T(8,128)S(1)}, u32[]{:S(2)}, u32[]{:S(2)}) async-start(f32[4,32,128]{2,1,0:T(8,128)} %broadcast_in_dim.52), calls=%async_computation.3 | async-start | bytes 131072 | tf_op jit(solution)/shard_map/all_to_all | solution.py:18
  425.9 18.1 %copy-start.6 = (f32[2]{0:T(128)}, f32[2]{0:T(128)S(1)}, u32[]{:S(2)}) copy-start(f32[2]{0:T(128)S(1)} %broadcast_multiply_fusion) | copy-start | bytes 28
  426.8 16.5 %all-to-all-start.4 = ((f32[64,8,2]{1,2,0:T(2,128)}), f32[64,8,2]{1,2,0:T(2,128)S(1)}, u32[]{:S(2)}, u32[]{:S(2)}) async-start(f32[64,8,2]{1,2,0:T(2,128)} %bitcast.25), calls=%async_computation.4 | async-start | bytes 131072 | tf_op jit(solution)/shard_map/all_to_all | solution.py:34
Sparse Core Ops, SparseCore 0:
  10.7 83.7 all-gather.1
where the time goes:
time: 452 us; the launch traced here: 451 us
  waiting for transfers between devices  314 us (69%)
  local copies, waits for them, and re-layouts  41.5 us (9%)
  starting transfers between devices  35.3 us (8%)
  other arithmetic  23.2 us (5%)
  matrix products  22.4 us (5%)
  between operations  14.4 us (3%)
    all_to_all x1, waiting for transfers between devices, per_device(): lax.all_to_all(sent[0], 'dp', split_axis=0, concat_axis=0, tiled=True)  222 us
    all_gather x1, waiting for transfers between devices, per_device(): all_queries = lax.all_gather(queries, 'dp', axis=0, tiled=True)  74.8 us
    reduce_sum x1, other arithmetic, fold_sources(): jnp.sum(summed_scores * factor[..., None], axis=0)  14.3 us
    all_to_all x1, starting transfers between devices, per_device(): lax.all_to_all(sent[0], 'dp', split_axis=0, concat_axis=0, tiled=True)  10.6 us
    unnamed x20, local copies, waits for them, and re-layouts  10.2 us
  transfers between devices with their start and end apart: 6, of which 5 were waited for; matrix products, arithmetic and copies ran while one was open for 10% of the time, Pallas kernels for 0%

commit v1 on v0

v1 whole, which is shorter than its diff:
```python
import functools

import jax
import jax.numpy as jnp
from jax import lax
from jax.experimental import pallas as pl
from jax.experimental.pallas import tpu as pltpu
from jax.sharding import PartitionSpec as P

HEAD_SIZE = 128
NCAND = 128
SAMPLES = 16
SPAN = 16
GROUP = 5
ROWS = SPAN * GROUP
WIDE = GROUP * HEAD_SIZE
SLOTS = 48
EMPTY = SLOTS
OWN = SLOTS + 1
NX, NZ, NY = 4, 8, 4
big_neg = -1e30
SCALE = HEAD_SIZE ** (-0.5)
F32 = jnp.float32
BF16 = jnp.bfloat16

ARRIVALS = [
    (1, 0, 0), (0, 0, 0), (1, 0, -1), (1, 0, 1), (1, -1, 0), (1, 1, 0), (0, -1, 0), (0, 1, 0),
    (0, 0, -1), (0, 0, 1), (1, 0, -2), (1, -1, -1), (1, 1, -1), (1, 0, 2), (1, -1, 1), (1, 1, 1),
    (0, -1, -1), (0, -1, 1), (1, -2, 0), (0, 1, -1), (0, 1, 1), (0, -2, 0), (0, 0, -2), (0, 0, 2),
    (1, 1, -2), (1, 0, -3), (1, -1, -2), (1, 0, 3), (1, 1, 2), (1, -2, -1), (0, -1, -2), (0, -1, 2),
    (1, -1, 2), (0, 1, -2), (0, 1, 2), (1, -2, 1), (0, -2, -1), (0, -2, 1), (1, 1, -3), (0, 0, -3),
    (0, 0, 3), (1, -1, -3), (1, 1, 3), (1, 0, -4), (1, -2, -2), (0, -1, 3), (1, -1, 3), (0, -1, -3),
    (0, 1, 3), (1, -2, 2), (0, 1, -3), (0, -2, 2), (0, -2, -2), (1, -2, -3), (1, 1, -4), (0, 0, -4),
    (1, -1, -4), (1, -2, 3), (0, -1, -4), (0, -2, 3), (0, 1, -4), (0, -2, -3), (1, -2, -4), (0, -2, -4),
]
UNIT = {key: i for i, key in enumerate(ARRIVALS)}
MOVES = {"x+": (-1, 0), "x-": (1, 0), "z+": (0, -1), "z-": (0, 1)}


def onward(key):
    head, xr, zr = key
    out = []
    if head == 0 or xr == 0:
        if -4 < zr <= 0:
            out.append("z+")
        if 0 <= zr < 3:
            out.append("z-")
    if head == 1 or zr == 0:
        if -2 < xr <= 0:
            out.append("x+")
        if 0 <= xr < 1:
            out.append("x-")
    return out


STAGE1 = [(0, "L", k, 0) for k in (4, 3, 2, 1)] + [(0, "S", k, 0) for k in (3, 2, 1)]
STAGE1 += [(1, "L", k, half) for k in (2, 1) for half in (0, 1)] + [(1, "S", 1, half) for half in (0, 1)]
STAGE2 = [(0, "L", 2), (0, "L", 1), (0, "S", 1)]
STAGE2 += [(1, "L", k) for k in (4, 3, 2, 1)] + [(1, "S", k) for k in (3, 2, 1)]
MSG1 = {key: i for i, key in enumerate(STAGE1)}
MSG2 = {key: i for i, key in enumerate(STAGE2)}


def kernel(
    q_ref, idx_s, idx_v, ans_s, kv_hbm, span_ref, w_ref,
    att_ref, score_ref, tally_ref,
    g0, g1, kv, sbuf, res, dm, dl, spst, fscr,
    sib_s, sib_ss, sib_r, sib_rs, m1_s, m1_ss, m1_r, m1_rs, m2_s, m2_ss, m2_r, m2_rs,
    r0, r0s, r1, r1s, lg, tc, tx, tz,
    kv_sem, own_sem, ag_send, ag_recv, sg_send, sg_recv,
    sib_send, sib_recv, m1_send, m1_recv, m2_send, m2_recv, tail_send, tail_recv,
):
    dp = lax.axis_index("dp")
    y = lax.axis_index("mp")
    core = dp % 2
    z = (dp // 2) % NZ
    x = dp // (2 * NZ)
    s = 1 - 2 * core
    other = 1 - core

    def device(xx, zz, cc, yy):
        return (xx * (2 * NZ) + zz * 2 + cc, yy)

    def along_x(k):
        return (x + s * k + 2 * NX) % NX

    def along_z(k):
        return (z + s * k + 2 * NZ) % NZ

    sibling = device(x, z, other, y)
    link = {
        "x+": device(along_x(1), z, core, y),
        "x-": device(along_x(-1), z, core, y),
        "z+": device(x, along_z(1), core, y),
        "z-": device(x, along_z(-1), core, y),
    }
    started = []

    def send(src, dst, ssem, rsem, dev):
        copy = pltpu.make_async_remote_copy(
            src_ref=src, dst_ref=dst, send_sem=ssem, recv_sem=rsem,
            device_id=dev, device_id_type=pl.DeviceIdType.MESH,
        )
        copy.start()
        started.append(copy)

    def arrived(dst, ssem, rsem):
        pltpu.make_async_remote_copy(
            src_ref=dst, dst_ref=dst, send_sem=ssem, recv_sem=rsem,
            device_id=sibling, device_id_type=pl.DeviceIdType.MESH,
        ).wait_recv()

    kv_copy = pltpu.make_async_copy(kv_hbm, kv, kv_sem)
    kv_copy.start()
    peers = [sibling]
    peers += [device((x + d) % NX, z, core, y) for d in range(1, NX)]
    peers += [device(x, (z + d) % NZ, core, y) for d in range(1, NZ)]
    peers += [device(x, z, core, (y + d) % NY) for d in range(1, NY)]
    barrier = pltpu.get_barrier_semaphore()
    for peer in peers:
        pl.semaphore_signal(barrier, inc=1, device_id=peer, device_id_type=pl.DeviceIdType.MESH)
    pl.semaphore_wait(barrier, len(peers))

    gathered = (g0, g1)

    def unit_row(key):
        head, xr, zr = key
        xx, zz = along_x(xr), along_z(zr)
        if head == 0:
            return ((core * NZ + zz) * NX + xx) * 2
        return ((core * NX + xx) * NZ + zz) * 2

    count = 0
    done = {}
    own_copies = []
    for key in ARRIVALS:
        head, xr, zr = key
        here = gathered[head].at[pl.ds(unit_row(key), 2)]
        if xr == 0 and zr == 0:
            src = q_ref.at[:, :, pl.ds(head * WIDE, WIDE)]
        else:
            arrived(here, ag_send.at[0], ag_recv.at[UNIT[key]])
            src = here
        for move in onward(key):
            dx, dz = MOVES[move]
            there = UNIT[(head, xr + dx, zr + dz)]
            send(src, here, ag_send.at[count], ag_recv.at[there], link[move])
            count += 1
        if xr == 0 and zr == 0:
            for c in range(2):
                gathered[head][unit_row(key) + c] = q_ref[c, :, head * WIDE : (head + 1) * WIDE]
        bundle = (head, zr if head == 0 else xr)
        done[bundle] = done.get(bundle, 0) + 1
        if head == 0 and done[bundle] == NX:
            zz = along_z(zr)
            rows = g0.at[pl.ds((core * NZ + zz) * NX * 2, NX * 2)]
            send(rows, rows, sg_send.at[zz], sg_recv.at[zz], sibling)
        if head == 1 and done[bundle] == NZ:
            xx = along_x(xr)
            rows = g1.at[pl.ds((core * NX + xx) * NZ * 2, NZ * 2)]
            send(rows, rows, sg_send.at[NZ + xx], sg_recv.at[NZ + xx], sibling)
    for zz in range(NZ):
        rows = g0.at[pl.ds((other * NZ + zz) * NX * 2, NX * 2)]
        arrived(rows, sg_send.at[zz], sg_recv.at[zz])
    for xx in range(NX):
        rows = g1.at[pl.ds((other * NX + xx) * NZ * 2, NZ * 2)]
        arrived(rows, sg_send.at[NZ + xx], sg_recv.at[NZ + xx])
    kv_copy.wait()

    lanes = lax.broadcasted_iota(jnp.int32, (ROWS, 128), 1)

    def query_rows(tile):
        return jnp.concatenate([tile[:, g * 128 : (g + 1) * 128] for g in range(GROUP)], axis=0)

    def score_block(b, carry):
        out = []
        for h in range(2):
            q = query_rows(gathered[h][idx_s[h, b]])
            k = kv[b, 0, :, h * 128 : (h + 1) * 128]
            sc = lax.dot_general(q, k, (((1,), (1,)), ((), ())), preferred_element_type=F32) * SCALE
            sbuf[b, h] = sc
            out.append(jnp.where(lanes == b, jnp.max(sc, axis=1, keepdims=True), carry[h]))
        return tuple(out)

    UNROLL = 4

    def score_step(i, carry):
        for u in range(UNROLL):
            carry = score_block(i * UNROLL + u, carry)
        return carry

    tops = lax.fori_loop(0, SLOTS // UNROLL, score_step, (jnp.full((ROWS, 128), big_neg, F32),) * 2)

    square = lax.broadcasted_iota(jnp.int32, (128, 128), 0)

    def pick(mat, row):
        hot = (square == idx_v[row : row + 1, :]).astype(F32)
        return jnp.dot(mat, hot, precision=lax.Precision.HIGHEST, preferred_element_type=F32)

    tops = tuple(jnp.maximum(t, pick(t, 6)) for t in tops)

    def weigh_block(b, carry):
        out = []
        for h in range(2):
            top = jnp.sum(jnp.where(lanes == b, tops[h], 0.0), axis=1, keepdims=True)
            wt = jnp.exp(sbuf[b, h] - top)
            out.append(jnp.where(lanes == b, jnp.sum(wt, axis=1, keepdims=True), carry[h]))
            v = kv[b, 1, :, h * 128 : (h + 1) * 128]
            res[b, h] = jnp.dot(wt.astype(BF16), v, preferred_element_type=F32)
        return tuple(out)

    def weigh_step(i, carry):
        for u in range(UNROLL):
            carry = weigh_block(i * UNROLL + u, carry)
        return carry

    sums = lax.fori_loop(0, SLOTS // UNROLL, weigh_step, (jnp.zeros((ROWS, 128), F32),) * 2)

    def as_rows(mat):
        return jnp.concatenate([mat, jnp.zeros((128 - ROWS, 128), F32)], axis=0).T

    for h in range(2):
        res[EMPTY, h] = jnp.zeros((ROWS, 128), F32)
        dm[h] = as_rows(pick(tops[h], 2 + 2 * h)).reshape(16, 8, 128)
        dl[h] = as_rows(pick(sums[h], 2 + 2 * h) + pick(sums[h], 3 + 2 * h)).reshape(16, 8, 128)

    def merge(n, sources, emit, normal=False):
        top = sources[0][1]
        for _, m, _ in sources[1:]:
            top = jnp.maximum(top, m)
        total = None
        for i, (_, m, l) in enumerate(sources):
            f = jnp.exp(m - top)
            fscr[i * n : (i + 1) * n, :] = f
            total = l * f if total is None else total + l * f
        width = len(sources) * n
        if normal:
            fscr[width : width + n, :] = 1.0 / total
            width += n
        width = (width + 7) // 8 * 8
        cols = fscr[0:width, :].T
        for j in range(n):
            acc = None
            for i, (load, _, _) in enumerate(sources):
                term = load(j) * cols[:ROWS, i * n + j : i * n + j + 1]
                acc = term if acc is None else acc + term
            if normal:
                at = len(sources) * n + j
                acc = acc * cols[:ROWS, at : at + 1]
            emit(j, acc)
        return top, total

    def held(h, cc, g):
        group = cc * 8 + g

        def load(j):
            at = group * 8 + j
            return res[idx_s[2 + 2 * h, at], h] + res[idx_s[3 + 2 * h, at], h]

        return load, dm[h, group], dl[h, group]

    def group_at(h, k, half):
        return along_z(k) if h == 0 else along_x(k) * 2 + half

    order = []
    for k in (4, 3, -3, 2, -2, 1, -1, 0):
        order.append((0, k, 0))
        if k in (4, 3):
            order += [(1, 2, 0), (1, 2, 1)] if k == 4 else [(1, 1, 0), (1, 1, 1)]
        if k == -3:
            order += [(1, -1, 0), (1, -1, 1)]
        if k == 2:
            order += [(1, 0, 0), (1, 0, 1)]
    for h, k, half in order:
        g = group_at(h, k, half)
        load, m, l = held(h, other, g)
        at = h * 8 + g
        for j in range(8):
            sib_s[at, j] = load(j).astype(BF16)
        sib_ss[at, 0:8, :] = m
        sib_ss[at, 8:16, :] = l
        send(sib_ss.at[at], sib_rs.at[at], sib_send.at[16 + at], sib_recv.at[16 + at], sibling)
        send(sib_s.at[at], sib_r.at[at], sib_send.at[at], sib_recv.at[at], sibling)

    keys = lax.broadcasted_iota(jnp.int32, (ROWS, SPAN), 1)
    tokens = lax.broadcasted_iota(jnp.int32, (ROWS, SPAN), 0) % SPAN
    for h in range(2):
        stat = jnp.zeros((ROWS, 128), F32)
        for c in range(2):
            q = query_rows(q_ref[c, :, h * WIDE : (h + 1) * WIDE])
            k = span_ref[c, 0, :, h * 128 : (h + 1) * 128]
            v = span_ref[c, 1, :, h * 128 : (h + 1) * 128]
            sc = lax.dot_general(q, k, (((1,), (1,)), ((), ())), preferred_element_type=F32) * SCALE
            sc = jnp.where(tokens >= keys, sc, big_neg)
            top = jnp.max(sc, axis=1, keepdims=True)
            wt = jnp.exp(sc - top)
            stat = jnp.where(lanes == c, top, stat)
            stat = jnp.where(lanes == 2 + c, jnp.sum(wt, axis=1, keepdims=True), stat)
            res[OWN + c, h] = jnp.dot(wt.astype(BF16), v, preferred_element_type=F32)
        spst[h] = as_rows(stat)[0:8, :]

    seen = set()

    def from_sibling(h, g):
        at = h * 8 + g
        arrived(sib_rs.at[at], sib_send.at[16 + at], sib_recv.at[16 + at])
        arrived(sib_r.at[at], sib_send.at[at], sib_recv.at[at])
        return (lambda j: sib_r[at, j].astype(F32)), sib_rs[at, 0:8, :], sib_rs[at, 8:16, :]

    def from_ring1(key):
        at = MSG1[key]
        arrived(m1_rs.at[at], m1_send.at[at, 1], m1_recv.at[at, 1])
        arrived(m1_r.at[at], m1_send.at[at, 0], m1_recv.at[at, 0])
        return (lambda j: m1_r[at, j].astype(F32)), m1_rs[at, 0:8, :], m1_rs[at, 8:16, :]

    def from_ring2(key):
        at = MSG2[key]
        arrived(m2_rs.at[at], m2_send.at[at, 1], m2_recv.at[at, 1])
        arrived(m2_r.at[at], m2_send.at[at, 0], m2_recv.at[at, 0])
        return (lambda j: m2_r[at, j].astype(F32)), m2_rs[at, 0:2, :], m2_rs[at, 2:4, :]

    def ring1(h, arm, k, half):
        at = MSG1[(h, arm, k, half)]
        sign = 1 if arm == "L" else -1
        g = group_at(h, sign * k, half)
        sources = [held(h, core, g), from_sibling(h, g)]
        if (h, arm, k + 1, half) in MSG1:
            sources.append(from_ring1((h, arm, k + 1, half)))

        def emit(j, acc):
            m1_s[at, j] = acc.astype(BF16)

        m, l = merge(8, sources, emit)
        m1_ss[at, 0:8, :] = m
        m1_ss[at, 8:16, :] = l
        dev = link[("z" if h == 0 else "x") + ("+" if arm == "L" else "-")]
        send(m1_ss.at[at], m1_rs.at[at], m1_send.at[at, 1], m1_recv.at[at, 1], dev)
        send(m1_s.at[at], m1_r.at[at], m1_send.at[at, 0], m1_recv.at[at, 0], dev)

    def home1(h, half):
        g = group_at(h, 0, half)
        sources = [held(h, core, g), from_sibling(h, g)]
        sources += [from_ring1((h, "L", 1, half)), from_ring1((h, "S", 1, half))]
        acc_ref, stat_ref = (r0, r0s) if h == 0 else (r1, r1s)

        def emit(j, acc):
            acc_ref[half * 8 + j] = acc

        m, l = merge(8, sources, emit)
        for i in range(4):
            stat_ref[half * 4 + i, 0:2, :] = m[2 * i : 2 * i + 2, :]
            stat_ref[half * 4 + i, 2:4, :] = l[2 * i : 2 * i + 2, :]
            stat_ref[half * 4 + i, 4:8, :] = jnp.zeros((4, 128), F32)

    def reduced(h, pos):
        acc_ref, stat_ref = (r0, r0s) if h == 0 else (r1, r1s)
        return (lambda j: acc_ref[pos * 2 + j]), stat_ref[pos, 0:2, :], stat_ref[pos, 2:4, :]

    def ring2(h, arm, k):
        at = MSG2[(h, arm, k)]
        sign = 1 if arm == "L" else -1
        pos = along_x(sign * k) if h == 0 else along_z(sign * k)
        source = reduced(h, pos)
        m2_ss[at, 4:8, :] = jnp.zeros((4, 128), F32)
        if (h, arm, k + 1) in MSG2:

            def emit(j, acc):
                m2_s[at, j] = acc.astype(BF16)

            m, l = merge(2, [source, from_ring2((h, arm, k + 1))], emit)
        else:
            for j in range(2):
                m2_s[at, j] = source[0](j).astype(BF16)
            m, l = source[1], source[2]
        m2_ss[at, 0:2, :] = m
        m2_ss[at, 2:4, :] = l
        dev = link[("x" if h == 0 else "z") + ("+" if arm == "L" else "-")]
        send(m2_ss.at[at], m2_rs.at[at], m2_send.at[at, 1], m2_recv.at[at, 1], dev)
        send(m2_s.at[at], m2_r.at[at], m2_send.at[at, 0], m2_recv.at[at, 0], dev)

    def home2(h):
        span = (lambda j: res[OWN + j, h]), spst[h, 0:2, :], spst[h, 2:4, :]
        pos = x if h == 0 else z
        sources = [reduced(h, pos), from_ring2((h, "L", 1)), from_ring2((h, "S", 1)), span]

        def emit(j, acc):
            for g in range(GROUP):
                col = h * WIDE + g * 128
                att_ref[j, :, col : col + 128] = acc[g * SPAN : (g + 1) * SPAN, :].astype(BF16)

        merge(2, sources, emit, normal=True)

    ring1(0, "L", 4, 0)
    ring1(1, "L", 2, 0)
    ring1(1, "L", 2, 1)
    ring1(0, "S", 3, 0)
    ring1(1, "S", 1, 0)
    ring1(1, "S", 1, 1)
    ring1(0, "L", 3, 0)
    ring1(1, "L", 1, 0)
    ring1(1, "L", 1, 1)
    ring1(0, "S", 2, 0)
    ring1(0, "L", 2, 0)
    home1(1, 0)
    home1(1, 1)
    ring2(1, "L", 4)
    ring2(1, "S", 3)
    ring1(0, "S", 1, 0)
    ring2(1, "L", 3)
    ring2(1, "S", 2)
    ring1(0, "L", 1, 0)
    ring2(1, "L", 2)
    ring2(1, "S", 1)
    home1(0, 0)
    ring2(0, "L", 2)
    ring2(0, "S", 1)
    ring2(1, "L", 1)
    ring2(0, "L", 1)
    home2(1)
    home2(0)

    def bits(ref, src_at, dst_at, sem, dev):
        send(ref.at[src_at], ref.at[dst_at], tail_send.at[sem], tail_recv.at[sem], dev)

    for c in range(2):
        lg[y, c * SPAN : (c + 1) * SPAN, :] = jnp.dot(
            att_ref[c], w_ref[...], preferred_element_type=F32
        )
    for d in range(1, NY):
        bits(lg, y, y, d - 1, device(x, z, core, (y + d) % NY))
    for d in range(1, NY):
        arrived(lg.at[(y + NY - d) % NY], tail_send.at[d - 1], tail_recv.at[d - 1])
    logits = lg[0] + lg[1] + lg[2] + lg[3]
    peak = jnp.max(logits, axis=1, keepdims=True)
    norm = peak + jnp.log(jnp.sum(jnp.exp(logits - peak), axis=1, keepdims=True))
    cand = lax.broadcasted_iota(jnp.int32, (SPAN, NCAND), 1)
    prompt_row = lax.broadcasted_iota(jnp.int32, (8, NCAND), 0)
    cand8 = lax.broadcasted_iota(jnp.int32, (8, NCAND), 1)
    tally = jnp.zeros((8, NCAND), F32)
    for c in range(2):
        rows = slice(c * SPAN, (c + 1) * SPAN)
        chosen = jnp.sum(jnp.where(cand == ans_s[c], logits[rows], 0.0), axis=1, keepdims=True)
        score = jnp.sum(chosen - norm[rows]) * (1.0 / SPAN)
        score_ref[c] = score
        prompt = (dp * 2 + c) // SAMPLES
        tally = tally + jnp.where((prompt_row == prompt) & (cand8 == ans_s[c]), score, 0.0)
    tc[core] = tally
    bits(tc, core, core, 3, sibling)
    arrived(tc.at[other], tail_send.at[3], tail_recv.at[3])
    tx[x] = tc[0] + tc[1]
    for d in range(1, NX):
        bits(tx, x, x, 3 + d, device((x + d) % NX, z, core, y))
    for d in range(1, NX):
        arrived(tx.at[(x + NX - d) % NX], tail_send.at[3 + d], tail_recv.at[3 + d])
    tz[z] = tx[0] + tx[1] + tx[2] + tx[3]
    for d in range(1, NZ):
        bits(tz, z, z, 6 + d, device(x, (z + d) % NZ, core, y))
    for d in range(1, NZ):
        arrived(tz.at[(z + NZ - d) % NZ], tail_send.at[6 + d], tail_recv.at[6 + d])
    whole = tz[0]
    for i in range(1, NZ):
        whole = whole + tz[i]
    for j in range(2):
        tally_ref[:, j : j + 1] = jnp.sum(
            jnp.where(cand8 == dp * 2 + j, whole, 0.0), axis=1, keepdims=True
        )
    for copy in started:
        copy.wait_send()


def tables(tags):
    e = jnp.arange(128, dtype=jnp.int32)
    c = e % 2
    core = e // 64
    chain0 = ((((e // 2) % NX) * NZ + (e // 8) % NZ) * 2 + core) * 2 + c
    chain1 = ((((e // 16) % NX) * NZ + (e // 2) % NZ) * 2 + core) * 2 + c
    padded = jnp.pad(tags, (0, 128 - SLOTS), constant_values=-1)
    tc, tcore, tz, tx = padded % 2, (padded // 2) % 2, (padded // 4) % NZ, padded // (4 * NZ)
    e0 = ((tcore * NZ + tz) * NX + tx) * 2 + tc
    e1 = ((tcore * NX + tx) * NZ + tz) * 2 + tc
    block = jnp.arange(128, dtype=jnp.int32)[None, :]

    def two(chain):
        hit = padded[None, :] == chain[:, None]
        first = jnp.min(jnp.where(hit, block, EMPTY), axis=1)
        second = jnp.max(jnp.where(hit, block, -1), axis=1)
        return first, jnp.where(second > first, second, EMPTY)

    f0, s0 = two(chain0)
    f1, s1 = two(chain1)
    twin = (padded[None, :] == padded[:, None]) & (block != e[:, None]) & (block < SLOTS)
    partner = jnp.max(jnp.where(twin, block, -1), axis=1)
    partner = jnp.where((partner < 0) | (e >= SLOTS), e, partner)
    return jnp.stack([e0, e1, f0, s0, f1, s1, partner, e])


def per_device(queries, key_value_cache, slot_tags, span_key_value, answer_id, w_cand):
    idx = tables(slot_tags)
    vmem = pl.BlockSpec(memory_space=pltpu.VMEM)
    smem = pl.BlockSpec(memory_space=pltpu.SMEM)
    unit = (8, ROWS, 128)
    stat = (16, 128)
    dma = pltpu.SemaphoreType.DMA
    n1, n2 = len(STAGE1), len(STAGE2)
    sends = sum(len(onward(key)) for key in ARRIVALS)
    return pl.pallas_call(
        kernel,
        out_shape=(
            jax.ShapeDtypeStruct((2, SPAN, 2 * WIDE), BF16),
            jax.ShapeDtypeStruct((2,), F32),
            jax.ShapeDtypeStruct((8, 2), F32),
        ),
        in_specs=[vmem, smem, vmem, smem, pl.BlockSpec(memory_space=pl.ANY), vmem, vmem],
        out_specs=(vmem, smem, vmem),
        scratch_shapes=[
            pltpu.VMEM((128, SPAN, WIDE), BF16),
            pltpu.VMEM((128, SPAN, WIDE), BF16),
            pltpu.VMEM(key_value_cache.shape, BF16),
            pltpu.VMEM((SLOTS, 2, ROWS, 128), F32),
            pltpu.VMEM((SLOTS + 3, 2, ROWS, 128), F32),
            pltpu.VMEM((2, 16, 8, 128), F32),
            pltpu.VMEM((2, 16, 8, 128), F32),
            pltpu.VMEM((2, 8, 128), F32),
            pltpu.VMEM((128, 128), F32),
            pltpu.VMEM((16, *unit), BF16),
            pltpu.VMEM((16, *stat), F32),
            pltpu.VMEM((16, *unit), BF16),
            pltpu.VMEM((16, *stat), F32),
            pltpu.VMEM((n1, *unit), BF16),
            pltpu.VMEM((n1, *stat), F32),
            pltpu.VMEM((n1, *unit), BF16),
            pltpu.VMEM((n1, *stat), F32),
            pltpu.VMEM((n2, 2, ROWS, 128), BF16),
            pltpu.VMEM((n2, 8, 128), F32),
            pltpu.VMEM((n2, 2, ROWS, 128), BF16),
            pltpu.VMEM((n2, 8, 128), F32),
            pltpu.VMEM((8, ROWS, 128), F32),
            pltpu.VMEM((4, 8, 128), F32),
            pltpu.VMEM((16, ROWS, 128), F32),
            pltpu.VMEM((8, 8, 128), F32),
            pltpu.VMEM((NY, 2 * SPAN, NCAND), F32),
            pltpu.VMEM((2, 8, 128), F32),
            pltpu.VMEM((NX, 8, 128), F32),
            pltpu.VMEM((NZ, 8, 128), F32),
            dma, dma,
            dma((sends,)), dma((len(ARRIVALS),)), dma((NZ + NX,)), dma((NZ + NX,)),
            dma((32,)), dma((32,)), dma((n1, 2)), dma((n1, 2)), dma((n2, 2)), dma((n2, 2)),
            dma((14,)), dma((14,)),
        ],
        compiler_params=pltpu.CompilerParams(
            collective_id=0, has_side_effects=True, vmem_limit_bytes=60 * 1024 * 1024
        ),
        name="score_chains",
    )(queries, idx, idx, answer_id, key_value_cache, span_key_value, w_cand)


def solution(mesh):
    in_specs = (
        P("dp", None, "mp"),
        P("dp", None, None, "mp"),
        P("dp"),
        P("dp", None, None, "mp"),
        P("dp"),
        P("mp", None),
    )
    out_specs = (P("dp", None, "mp"), P("dp"), P(None, "dp"))
    return jax.shard_map(
        per_device, mesh=mesh, in_specs=in_specs, out_specs=out_specs, check_vma=False
    )
```

time: 452 us -> 102 us (0.23)
  waiting for transfers between devices: 314 us -> 0 us
  Pallas kernels: 0 us -> 95.5 us
  local copies, waits for them, and re-layouts: 41.5 us -> 4.57 us
  starting transfers between devices: 35.3 us -> 0 us
  matrix products: 22.4 us -> 0 us
  other arithmetic: 23.2 us -> 1 us
  between operations: 14.4 us -> 0.68 us
    all_to_all x5 -> x0, waiting for transfers between devices: 239 us -> none  [the longest x1 222 us: per_device(): lax.all_to_all(sent[0], 'dp', split_axis=0, concat_axis=0, tiled=True)]
    pallas_call x0 -> x1, Pallas kernels: none -> 95.5 us  [per_device(): pl.pallas_call(kernel, out_shape=(jax.ShapeDtypeStruct((2, SPAN, 2 * WIDE...]
    all_gather x1 -> x0, waiting for transfers between devices: 74.8 us -> none  [per_device(): all_queries = lax.all_gather(queries, 'dp', axis=0, tiled=True)]
    all_to_all x5 -> x0, starting transfers between devices: 35.3 us -> none  [the longest x1 10.6 us: per_device(): lax.all_to_all(sent[0], 'dp', split_axis=0, concat_axis=0, tiled=True)]
    dot_general x7 -> x0, matrix products: 21.9 us -> none  [the longest x1 8.68 us: merge_items(): jnp.einsum('nc,nkgad->ckgad', member_f, summed_scores * factor[..., None]...]
    reduce_sum x9 -> x0, other arithmetic: 19.4 us -> none  [the longest x1 14.3 us: fold_sources(): jnp.sum(summed_scores * factor[..., None], axis=0)]
    reshape x5 -> x0, local copies, waits for them, and re-layouts: 13.3 us -> none  [the longest x1 7.14 us: per_device(): chain_sum.reshape(grid + chain_sum.shape[1:])]
    unnamed x20 -> x2, local copies, waits for them, and re-layouts: 10.2 us -> 2.63 us
  transfers between devices with their start and end apart: 6 -> 0, of which waited for: 5 -> 0; matrix products, arithmetic and copies ran while one was open for 10% -> 0% of each run, Pallas kernels for 0% -> 0%
where the time goes in v1:
time: 102 us
  Pallas kernels  95.5 us (94%)
  local copies, waits for them, and re-layouts  4.57 us (4%)
    pallas_call x1, Pallas kernels, per_device(): pl.pallas_call(kernel, out_shape=(jax.ShapeDtypeStruct((2, SPAN, 2 * WIDE...  95.5 us
    unnamed x2, local copies, waits for them, and re-layouts  2.63 us

profile of v1, /device:TPU:1, one launch (start us, length us, event | category | flops | bytes accessed | tf_op | source)
XLA Modules:
  0.0 101.8 jit_solution(4607421776285265191)
XLA Ops:
  0.7 0.7 add_bitcast_fusion
  1.4 0.3 fusion.3
  1.7 0.6 stack.23.idx_s.idx_v
  2.3 95.5 %score_chains.1 = (bf16[2,16,1280]{2,1,0:T(8,128)(2,1)}, f32[2]{0:T(128)}, f32[8,2]{1,0:T(8,128)}) custom-call(bf16[2,16,1280]{2,1,0:T(8,128)(2,1)} %q_ref.1, s32[8,128]{1,0:T(8,128)} %stack.23.idx_s.idx_v, s32[8,128]{1,0:T(8,128)} %stack.23.idx_s.idx_v, s32[2]{0:T(128)} %ans_s.1, bf16[48,2,128,256]{3,2,1,0:T(8,128)(2,1)} %kv_hbm.1, ...), custom_call_target="tpu_custom_call" | custom-call | tf_op jit(solution)/shard_map/score_chains/pallas_call | solution.py:506
  97.8 1.3 %copy.10 = f32[8,2]{0,1:T(2,128)} copy(f32[8,2]{1,0:T(8,128)} %get-tuple-element.8) | data formatting | bytes 128 | tf_op jit(solution)/shard_map/score_chains/pallas_call | solution.py:506
  99.2 1.5 %copy.13 = bf16[2,16,1280]{2,1,0:T(8,128)(2,1)} copy(bf16[2,16,1280]{2,1,0:T(8,128)(2,1)} %get-tuple-element.27) | data formatting | bytes 163840
  100.7 1.1 %copy.14 = f32[2]{0:T(128)} copy(f32[2]{0:T(128)} %get-tuple-element.28) | data formatting | bytes 16
  (7 shorter events, 0.1 us)

commit v2 on v1

v2 whole, which is shorter than its diff:
```python
import jax
import jax.numpy as jnp
from jax import lax
from jax.experimental import pallas as pl
from jax.experimental.pallas import tpu as pltpu
from jax.sharding import PartitionSpec as P

HEAD_SIZE = 128
NCAND = 128
SAMPLES = 16
SPAN = 16
GROUP = 5
ROWS = SPAN * GROUP
WIDE = GROUP * HEAD_SIZE
SLOTS = 48
EMPTY = SLOTS
OWN = SLOTS + 1
NX, NZ, NY = 4, 8, 4
big_neg = -1e30
SCALE = HEAD_SIZE ** (-0.5)
F32 = jnp.float32
BF16 = jnp.bfloat16

ARRIVALS = [
    (0, 0, 0), (1, 0, 0), (0, -1, 0), (0, 0, -1), (0, 0, 1), (0, 1, 0), (1, 0, -1), (1, 0, 1),
    (1, 1, 0), (0, -2, 0), (1, 0, -2), (1, 0, 2), (1, -1, 0), (0, -1, -1), (0, -1, 1), (1, -1, -1),
    (1, 1, -1), (0, 0, -2), (0, 0, 2), (1, -1, 1), (1, 1, 1), (0, 1, -1), (0, 1, 1), (1, -1, -2),
    (1, 1, -2), (1, -1, 2), (1, 1, 2), (1, 0, -3), (1, 0, 3), (1, -2, 0), (0, -2, -1), (0, -2, 1),
    (1, -2, -1), (0, -1, 2), (1, -2, 1), (1, 0, -4), (0, 0, 3), (1, 1, -3), (1, -2, -2), (0, -1, -2),
    (0, 1, 2), (1, 1, 3), (1, -2, 2), (0, -2, 2), (0, 0, -3), (1, -1, -3), (0, -1, 3), (0, 1, -2),
    (1, 1, -4), (1, -1, 3), (0, -2, -2), (1, -1, -4), (0, 1, 3), (0, -1, -3), (0, -2, 3), (0, 0, -4),
    (1, -2, -3), (0, 1, -3), (1, -2, 3), (0, -2, -3), (1, -2, -4), (0, -1, -4), (0, 1, -4), (0, -2, -4),
]
UNIT = {key: i for i, key in enumerate(ARRIVALS)}
MOVES = {
    "x+": (-1, 0), "x-": (1, 0), "z+": (0, -1), "z-": (0, 1),
    "x++": (-2, 0), "z++": (0, -2), "z--": (0, 2),
}


def onward(key):
    head, xr, zr = key
    out = []
    if head == 1:
        if xr == 0:
            if zr == 0:
                out += ["z+", "z-", "z++", "z--"]
            if zr in (-1, -2):
                out.append("z++")
            if zr == 1:
                out.append("z--")
        if -2 < xr <= 0:
            out.append("x+")
        if 0 <= xr < 1:
            out.append("x-")
    else:
        if -4 < zr <= 0:
            out.append("z+")
        if 0 <= zr < 3:
            out.append("z-")
        if xr == 0 and zr == 0:
            out += ["x+", "x-", "x++"]
    return out


STAGE1 = [(0, arm, k, half) for arm, top in (("L", 4), ("S", 3)) for k in range(1, top + 1) for half in (0, 1)]
STAGE1 += [(1, arm, k, half) for arm, top in (("L", 2), ("S", 1)) for k in range(1, top + 1) for half in (0, 1)]
STAGE2 = {
    (0, "L", 2): ("x++", None), (0, "L", 1): ("x+", None), (0, "S", 1): ("x-", None),
    (1, "L", 4): ("z++", None), (1, "L", 3): ("z++", None),
    (1, "S", 3): ("z--", None), (1, "S", 2): ("z--", None),
    (1, "L", 2): ("z++", (1, "L", 4)), (1, "L", 1): ("z+", (1, "L", 3)), (1, "S", 1): ("z-", (1, "S", 3)),
}
LAST = ([("L", 2), ("L", 1), ("S", 1)], [("L", 2), ("L", 1), ("S", 1), ("S", 2)])
MSG1 = {key: i for i, key in enumerate(STAGE1)}
MSG2 = {key: i for i, key in enumerate(STAGE2)}
STEPS = [
    ("sb", 0, 4, 0), ("sb", 1, 2, 0), ("sb", 1, 2, 1), ("sb", 0, -3, 0),
    ("sb", 0, 3, 0), ("sb", 0, -2, 0), ("r1", 0, "L", 4, 0), ("r1", 0, "L", 4, 1),
    ("r1", 1, "L", 2, 0), ("r1", 1, "L", 2, 1), ("sb", 0, 2, 0), ("r1", 0, "S", 3, 0),
    ("r1", 0, "S", 3, 1), ("sb", 1, -1, 0), ("sb", 1, -1, 1), ("sb", 1, 1, 0),
    ("sb", 1, 1, 1), ("sb", 0, -1, 0), ("sb", 0, 1, 0), ("sb", 0, 0, 0),
    ("sb", 1, 0, 0), ("sb", 1, 0, 1), ("r1", 1, "S", 1, 0), ("r1", 1, "S", 1, 1),
    ("r1", 0, "L", 3, 0), ("r1", 0, "S", 2, 0), ("r1", 0, "L", 3, 1), ("r1", 1, "L", 1, 0),
    ("r1", 0, "S", 2, 1), ("r1", 0, "L", 2, 0), ("r1", 0, "S", 1, 0), ("r1", 1, "L", 1, 1),
    ("r1", 0, "L", 2, 1), ("r1", 0, "S", 1, 1), ("r1", 0, "L", 1, 0), ("h1", 1, 0),
    ("r1", 0, "L", 1, 1), ("h1", 1, 1), ("r2", 1, "L", 4), ("r2", 1, "L", 3),
    ("r2", 1, "S", 3), ("r2", 1, "S", 2), ("h1", 0, 0), ("h1", 0, 1),
    ("r2", 0, "L", 2), ("r2", 0, "L", 1), ("r2", 0, "S", 1), ("r2", 1, "L", 2),
    ("r2", 1, "S", 1), ("r2", 1, "L", 1), ("h2", 0), ("h2", 1),
]


def kernel(
    q_hbm, idx_s, idx_v, ans_s, kv_hbm, span_hbm, w_hbm,
    att_ref, small_ref,
    q_ref, span_ref, w_ref, ring_tally,
    g0, g1, kv, sbuf, res, dm, dl, spst, fscr,
    sib_s, sib_ss, sib_r, sib_rs, m1_s, m1_ss, m1_r, m1_rs, m2_s, m2_ss, m2_r, m2_rs,
    r0, r0s, r1, r1s, lg, ta, tz,
    in_sem, ag_send, ag_recv, sg_send, sg_recv,
    sib_send, sib_recv, m1_send, m1_recv, m2_send, m2_recv, tail_send, tail_recv,
):
    dp = lax.axis_index("dp")
    y = lax.axis_index("mp")
    core = dp % 2
    z = (dp // 2) % NZ
    x = dp // (2 * NZ)
    s = 1 - 2 * core
    other = 1 - core

    def device(xx, zz, cc, yy):
        return (xx * (2 * NZ) + zz * 2 + cc, yy)

    def along_x(k):
        return (x + s * k + 2 * NX) % NX

    def along_z(k):
        return (z + s * k + 2 * NZ) % NZ

    sibling = device(x, z, other, y)
    link = {
        "x+": device(along_x(1), z, core, y),
        "x-": device(along_x(-1), z, core, y),
        "z+": device(x, along_z(1), core, y),
        "z-": device(x, along_z(-1), core, y),
        "x++": device(along_x(2), z, core, y),
        "z++": device(x, along_z(2), core, y),
        "z--": device(x, along_z(-2), core, y),
    }
    started = []

    def send(src, dst, ssem, rsem, dev):
        copy = pltpu.make_async_remote_copy(
            src_ref=src, dst_ref=dst, send_sem=ssem, recv_sem=rsem,
            device_id=dev, device_id_type=pl.DeviceIdType.MESH,
        )
        copy.start()
        started.append(copy)

    def arrived(dst, ssem, rsem):
        pltpu.make_async_remote_copy(
            src_ref=dst, dst_ref=dst, send_sem=ssem, recv_sem=rsem,
            device_id=sibling, device_id_type=pl.DeviceIdType.MESH,
        ).wait_recv()

    q_copy = pltpu.make_async_copy(q_hbm, q_ref, in_sem.at[0])
    kv_copy = pltpu.make_async_copy(kv_hbm, kv, in_sem.at[1])
    span_copy = pltpu.make_async_copy(span_hbm, span_ref, in_sem.at[2])
    w_copy = pltpu.make_async_copy(w_hbm, w_ref, in_sem.at[3])
    q_copy.start()
    peers = [sibling]
    peers += [device((x + d) % NX, z, core, y) for d in range(1, NX)]
    peers += [device(x, (z + d) % NZ, core, y) for d in (1, 2, NZ - 2, NZ - 1)]
    peers += [device(x, z, core, (y + d) % NY) for d in range(1, NY)]
    barrier = pltpu.get_barrier_semaphore()
    for peer in peers:
        pl.semaphore_signal(barrier, inc=1, device_id=peer, device_id_type=pl.DeviceIdType.MESH)
    span_copy.start()
    w_copy.start()
    q_copy.wait()
    pl.semaphore_wait(barrier, len(peers))

    gathered = (g0, g1)

    def unit_row(key):
        head, xr, zr = key
        xx, zz = along_x(xr), along_z(zr)
        if head == 0:
            return ((core * NZ + zz) * NX + xx) * 2
        return ((core * NX + xx) * NZ + zz) * 2

    lanes = lax.broadcasted_iota(jnp.int32, (ROWS, 128), 1)

    def query_rows(tile):
        return jnp.concatenate([tile[:, g * 128 : (g + 1) * 128] for g in range(GROUP)], axis=0)

    def as_rows(mat):
        return jnp.concatenate([mat, jnp.zeros((128 - ROWS, 128), F32)], axis=0).T

    def own_spans():
        span_copy.wait()
        keys = lax.broadcasted_iota(jnp.int32, (ROWS, SPAN), 1)
        tokens = lax.broadcasted_iota(jnp.int32, (ROWS, SPAN), 0) % SPAN
        for h in range(2):
            stat = jnp.zeros((ROWS, 128), F32)
            for c in range(2):
                q = query_rows(q_ref[c, :, h * WIDE : (h + 1) * WIDE])
                k = span_ref[c, 0, :, h * 128 : (h + 1) * 128]
                v = span_ref[c, 1, :, h * 128 : (h + 1) * 128]
                sc = lax.dot_general(q, k, (((1,), (1,)), ((), ())), preferred_element_type=F32) * SCALE
                sc = jnp.where(tokens >= keys, sc, big_neg)
                top = jnp.max(sc, axis=1, keepdims=True)
                wt = jnp.exp(sc - top)
                stat = jnp.where(lanes == c, top, stat)
                stat = jnp.where(lanes == 2 + c, jnp.sum(wt, axis=1, keepdims=True), stat)
                res[OWN + c, h] = jnp.dot(wt.astype(BF16), v, preferred_element_type=F32)
            spst[h] = as_rows(stat)[0:8, :]

    count = 0
    done = {}
    for step, key in enumerate(ARRIVALS):
        if step == 2:
            kv_copy.start()
        if step == 12:
            own_spans()
        head, xr, zr = key
        here = gathered[head].at[pl.ds(unit_row(key), 2)]
        if xr == 0 and zr == 0:
            src = q_ref.at[:, :, pl.ds(head * WIDE, WIDE)]
        else:
            arrived(here, ag_send.at[0], ag_recv.at[UNIT[key]])
            src = here
        for move in onward(key):
            dx, dz = MOVES[move]
            there = UNIT[(head, xr + dx, zr + dz)]
            send(src, here, ag_send.at[count], ag_recv.at[there], link[move])
            count += 1
        if xr == 0 and zr == 0:
            for c in range(2):
                gathered[head][unit_row(key) + c] = q_ref[c, :, head * WIDE : (head + 1) * WIDE]
        bundle = (head, zr if head == 0 else xr)
        done[bundle] = done.get(bundle, 0) + 1
        if head == 0 and done[bundle] == NX:
            zz = along_z(zr)
            rows = g0.at[pl.ds((core * NZ + zz) * NX * 2, NX * 2)]
            send(rows, rows, sg_send.at[zz], sg_recv.at[zz], sibling)
        if head == 1 and done[bundle] == NZ:
            xx = along_x(xr)
            rows = g1.at[pl.ds((core * NX + xx) * NZ * 2, NZ * 2)]
            send(rows, rows, sg_send.at[NZ + xx], sg_recv.at[NZ + xx], sibling)
    for zz in range(NZ):
        rows = g0.at[pl.ds((other * NZ + zz) * NX * 2, NX * 2)]
        arrived(rows, sg_send.at[zz], sg_recv.at[zz])
    for xx in range(NX):
        rows = g1.at[pl.ds((other * NX + xx) * NZ * 2, NZ * 2)]
        arrived(rows, sg_send.at[NZ + xx], sg_recv.at[NZ + xx])
    kv_copy.wait()

    def score_block(b, carry):
        out = []
        for h in range(2):
            q = query_rows(gathered[h][idx_s[h, b]])
            k = kv[b, 0, :, h * 128 : (h + 1) * 128]
            sc = lax.dot_general(q, k, (((1,), (1,)), ((), ())), preferred_element_type=F32) * SCALE
            sbuf[b, h] = sc
            out.append(jnp.where(lanes == b, jnp.max(sc, axis=1, keepdims=True), carry[h]))
        return tuple(out)

    UNROLL = 4

    def score_step(i, carry):
        for u in range(UNROLL):
            carry = score_block(i * UNROLL + u, carry)
        return carry

    tops = lax.fori_loop(0, SLOTS // UNROLL, score_step, (jnp.full((ROWS, 128), big_neg, F32),) * 2)

    square = lax.broadcasted_iota(jnp.int32, (128, 128), 0)

    def pick(mat, wanted):
        hot = (square == wanted).astype(F32)
        return jnp.dot(mat, hot, precision=lax.Precision.HIGHEST, preferred_element_type=F32)

    twin = idx_v[6:7, :]
    twin = jnp.where(twin < 0, lax.broadcasted_iota(jnp.int32, (1, 128), 1), twin)
    tops = tuple(jnp.maximum(t, pick(t, twin)) for t in tops)

    def weigh_block(b, carry):
        out = []
        for h in range(2):
            top = jnp.sum(jnp.where(lanes == b, tops[h], 0.0), axis=1, keepdims=True)
            wt = jnp.exp(sbuf[b, h] - top)
            out.append(jnp.where(lanes == b, jnp.sum(wt, axis=1, keepdims=True), carry[h]))
            v = kv[b, 1, :, h * 128 : (h + 1) * 128]
            res[b, h] = jnp.dot(wt.astype(BF16), v, preferred_element_type=F32)
        return tuple(out)

    def weigh_step(i, carry):
        for u in range(UNROLL):
            carry = weigh_block(i * UNROLL + u, carry)
        return carry

    sums = lax.fori_loop(0, SLOTS // UNROLL, weigh_step, (jnp.zeros((ROWS, 128), F32),) * 2)

    for h in range(2):
        res[EMPTY, h] = jnp.zeros((ROWS, 128), F32)
        first = EMPTY - idx_v[2 + 2 * h : 3 + 2 * h, :]
        last = idx_v[3 + 2 * h : 4 + 2 * h, :]
        last = jnp.where(last > first, last, EMPTY)
        dm[h] = as_rows(pick(tops[h], first)).reshape(16, 8, 128)
        dl[h] = as_rows(pick(sums[h], first) + pick(sums[h], last)).reshape(16, 8, 128)

    def merge(n, sources, emit, normal=False):
        top = sources[0][1]
        for _, m, _ in sources[1:]:
            top = jnp.maximum(top, m)
        total = None
        for i, (_, m, l) in enumerate(sources):
            f = jnp.exp(m - top)
            fscr[i * n : (i + 1) * n, :] = f
            total = l * f if total is None else total + l * f
        width = len(sources) * n
        if normal:
            fscr[width : width + n, :] = 1.0 / total
            width += n
        width = (width + 7) // 8 * 8
        cols = fscr[0:width, :].T
        for j in range(n):
            acc = None
            for i, (load, _, _) in enumerate(sources):
                term = load(j) * cols[:ROWS, i * n + j : i * n + j + 1]
                acc = term if acc is None else acc + term
            if normal:
                at = len(sources) * n + j
                acc = acc * cols[:ROWS, at : at + 1]
            emit(j, acc)
        return top, total

    def held(h, cc, g, first, n):
        group = cc * 8 + g

        def load(j):
            at = group * 8 + first + j
            one, two = EMPTY - idx_s[2 + 2 * h, at], idx_s[3 + 2 * h, at]
            return res[one, h] + res[jnp.where(two > one, two, EMPTY), h]

        return load, dm[h, group, first : first + n, :], dl[h, group, first : first + n, :]

    def group_at(h, k, half):
        return along_z(k) if h == 0 else along_x(k) * 2 + half

    def to_sibling(h, k, half):
        g = group_at(h, k, half)
        load, m, l = held(h, other, g, 0, 8)
        at = h * 8 + g
        for j in range(8):
            sib_s[at, j] = load(j).astype(BF16)
        sib_ss[at, 0:8, :] = m
        sib_ss[at, 8:16, :] = l
        send(sib_ss.at[at], sib_rs.at[at], sib_send.at[16 + at], sib_recv.at[16 + at], sibling)
        send(sib_s.at[at], sib_r.at[at], sib_send.at[at], sib_recv.at[at], sibling)

    seen = set()

    def from_sibling(h, g, key, first, n):
        at = h * 8 + g
        if key not in seen:
            seen.add(key)
            arrived(sib_rs.at[at], sib_send.at[16 + at], sib_recv.at[16 + at])
            arrived(sib_r.at[at], sib_send.at[at], sib_recv.at[at])
        stat = sib_rs[at, first : first + n, :], sib_rs[at, 8 + first : 8 + first + n, :]
        return (lambda j: sib_r[at, first + j].astype(F32)), *stat

    def from_ring1(key, n):
        at = MSG1[key]
        arrived(m1_rs.at[at, pl.ds(0, 2 * n)], m1_send.at[at, 1], m1_recv.at[at, 1])
        arrived(m1_r.at[at, pl.ds(0, n)], m1_send.at[at, 0], m1_recv.at[at, 0])
        return (lambda j: m1_r[at, j].astype(F32)), m1_rs[at, 0:n, :], m1_rs[at, n : 2 * n, :]

    def from_ring2(key):
        at = MSG2[key]
        arrived(m2_rs.at[at], m2_send.at[at, 1], m2_recv.at[at, 1])
        arrived(m2_r.at[at], m2_send.at[at, 0], m2_recv.at[at, 0])
        return (lambda j: m2_r[at, j].astype(F32)), m2_rs[at, 0:2, :], m2_rs[at, 2:4, :]

    def local(h, k, half):
        g = group_at(h, k, half)
        first, n = (half * 4, 4) if h == 0 else (0, 8)
        key = (h, k) if h == 0 else (h, k, half)
        return n, [held(h, core, g, first, n), from_sibling(h, g, key, first, n)]

    def ring1(h, arm, k, half):
        at = MSG1[(h, arm, k, half)]
        n, sources = local(h, k if arm == "L" else -k, half)
        if (h, arm, k + 1, half) in MSG1:
            sources.append(from_ring1((h, arm, k + 1, half), n))

        def emit(j, acc):
            m1_s[at, j] = acc.astype(BF16)

        m, l = merge(n, sources, emit)
        m1_ss[at, 0:n, :] = m
        m1_ss[at, n : 2 * n, :] = l
        dev = link[("z" if h == 0 else "x") + ("+" if arm == "L" else "-")]
        stat, data = pl.ds(0, 2 * n), pl.ds(0, n)
        send(m1_ss.at[at, stat], m1_rs.at[at, stat], m1_send.at[at, 1], m1_recv.at[at, 1], dev)
        send(m1_s.at[at, data], m1_r.at[at, data], m1_send.at[at, 0], m1_recv.at[at, 0], dev)

    def home1(h, half):
        n, sources = local(h, 0, half)
        sources += [from_ring1((h, "L", 1, half), n), from_ring1((h, "S", 1, half), n)]
        acc_ref, stat_ref = (r0, r0s) if h == 0 else (r1, r1s)

        def emit(j, acc):
            acc_ref[half * n + j] = acc

        m, l = merge(n, sources, emit)
        for i in range(n // 2):
            at = half * (n // 2) + i
            stat_ref[at, 0:2, :] = m[2 * i : 2 * i + 2, :]
            stat_ref[at, 2:4, :] = l[2 * i : 2 * i + 2, :]

    def reduced(h, pos):
        acc_ref, stat_ref = (r0, r0s) if h == 0 else (r1, r1s)
        return (lambda j: acc_ref[pos * 2 + j]), stat_ref[pos, 0:2, :], stat_ref[pos, 2:4, :]

    def ring2(h, arm, k):
        at = MSG2[(h, arm, k)]
        move, joins = STAGE2[(h, arm, k)]
        offset = k if arm == "L" else -k
        source = reduced(h, along_x(offset) if h == 0 else along_z(offset))
        if joins is None:
            for j in range(2):
                m2_s[at, j] = source[0](j).astype(BF16)
            m, l = source[1], source[2]
        else:

            def emit(j, acc):
                m2_s[at, j] = acc.astype(BF16)

            m, l = merge(2, [source, from_ring2(joins)], emit)
        m2_ss[at, 0:2, :] = m
        m2_ss[at, 2:4, :] = l
        m2_ss[at, 4:8, :] = jnp.zeros((4, 128), F32)
        send(m2_ss.at[at], m2_rs.at[at], m2_send.at[at, 1], m2_recv.at[at, 1], link[move])
        send(m2_s.at[at], m2_r.at[at], m2_send.at[at, 0], m2_recv.at[at, 0], link[move])

    def home2(h):
        span = (lambda j: res[OWN + j, h]), spst[h, 0:2, :], spst[h, 2:4, :]
        sources = [reduced(h, x if h == 0 else z), span]
        sources += [from_ring2((h, *last)) for last in LAST[h]]

        def emit(j, acc):
            for g in range(GROUP):
                col = h * WIDE + g * 128
                att_ref[j, :, col : col + 128] = acc[g * SPAN : (g + 1) * SPAN, :].astype(BF16)

        merge(2, sources, emit, normal=True)

    run = {"sb": to_sibling, "r1": ring1, "h1": home1, "r2": ring2, "h2": home2}
    for step in STEPS:
        run[step[0]](*step[1:])

    w_copy.wait()
    def bits(ref, src_at, dst_at, sem, dev):
        send(ref.at[src_at], ref.at[dst_at], tail_send.at[sem], tail_recv.at[sem], dev)

    for c in range(2):
        lg[y, c * SPAN : (c + 1) * SPAN, :] = jnp.dot(
            att_ref[c], w_ref[...], preferred_element_type=F32
        )
    for d in range(1, NY):
        bits(lg, y, y, d - 1, device(x, z, core, (y + d) % NY))
    for d in range(1, NY):
        arrived(lg.at[(y + NY - d) % NY], tail_send.at[d - 1], tail_recv.at[d - 1])
    logits = lg[0] + lg[1] + lg[2] + lg[3]
    peak = jnp.max(logits, axis=1, keepdims=True)
    norm = peak + jnp.log(jnp.sum(jnp.exp(logits - peak), axis=1, keepdims=True))
    cand = lax.broadcasted_iota(jnp.int32, (SPAN, NCAND), 1)
    prompt_row = lax.broadcasted_iota(jnp.int32, (8, NCAND), 0)
    cand8 = lax.broadcasted_iota(jnp.int32, (8, NCAND), 1)
    tally = jnp.zeros((8, NCAND), F32)
    scores = []
    for c in range(2):
        rows = slice(c * SPAN, (c + 1) * SPAN)
        chosen = jnp.sum(jnp.where(cand == ans_s[c], logits[rows], 0.0), axis=1, keepdims=True)
        score = jnp.sum(chosen - norm[rows]) * (1.0 / SPAN)
        scores.append(score)
        prompt = (dp * 2 + c) // SAMPLES
        tally = tally + jnp.where((prompt_row == prompt) & (cand8 == ans_s[c]), score, 0.0)
    here = x * 2 + core
    ta[here] = tally
    for d in range(1, 2 * NX):
        dx, dc = d // 2, d % 2
        dev = device((x + dx) % NX, z, (core + dc) % 2, y)
        bits(ta, here, here, 2 + d, dev)
    for d in range(1, 2 * NX):
        dx, dc = d // 2, d % 2
        source = (x + NX - dx) % NX * 2 + (core + dc) % 2
        arrived(ta.at[source], tail_send.at[2 + d], tail_recv.at[2 + d])
    part = ta[0]
    for i in range(1, 2 * NX):
        part = part + ta[i]
    tz[z] = part
    for d in range(1, NZ):
        bits(tz, z, z, 9 + d, device(x, (z + d) % NZ, core, y))
    for d in range(1, NZ):
        arrived(tz.at[(z + NZ - d) % NZ], tail_send.at[9 + d], tail_recv.at[9 + d])
    whole = tz[0]
    for i in range(1, NZ):
        whole = whole + tz[i]
    ring_tally[:, 0:8] = whole.T
    small_ref[0:2, :] = jnp.zeros((2, 128), F32)
    small_ref[0:2, 0:8] = ring_tally[pl.ds(dp * 2, 2), 0:8]
    row = lax.broadcasted_iota(jnp.int32, (2, 128), 0)
    small_ref[2:4, :] = jnp.where(row == 0, scores[0], scores[1])
    small_ref[4:8, :] = jnp.zeros((4, 128), F32)
    for copy in started:
        copy.wait_send()


def hand_out(att_ref, small_ref, out_ref, score_ref, tally_ref):
    out_ref[...] = att_ref[...]
    tally_ref[...] = small_ref[0:2, 0:8]
    score_ref[0] = small_ref[2, 0]
    score_ref[1] = small_ref[3, 0]


def tables(tags):
    r, e, b = (lax.broadcasted_iota(jnp.int32, (8, 128, 128), axis) for axis in range(3))
    c, core = e % 2, e // 64
    chain0 = ((((e // 2) % NX) * NZ + (e // 8) % NZ) * 2 + core) * 2 + c
    chain1 = ((((e // 16) % NX) * NZ + (e // 2) % NZ) * 2 + core) * 2 + c
    padded = jnp.pad(tags, (0, 128 - SLOTS), constant_values=-1)
    tag, mine = padded[None, None, :], padded[None, :, None]
    tc, tcore, tz, tx = tag % 2, (tag // 2) % 2, (tag // 4) % NZ, tag // (4 * NZ)
    place0 = ((tcore * NZ + tz) * NX + tx) * 2 + tc
    place1 = ((tcore * NX + tx) * NZ + tz) * 2 + tc
    wanted = jnp.where(r < 4, chain0, jnp.where(r < 6, chain1, mine))
    hit = jnp.where(r < 2, b == e, (tag == wanted) & ((r < 6) | (b != e))) & (b < SLOTS)
    first = (r == 2) | (r == 4)
    value = jnp.where(first, EMPTY - b, jnp.where(r == 0, place0, jnp.where(r == 1, place1, b)))
    return jnp.max(jnp.where(hit, value, jnp.where(first, 0, -1)), axis=2)


def per_device(queries, key_value_cache, slot_tags, span_key_value, answer_id, w_cand):
    idx = tables(slot_tags)
    vmem = pl.BlockSpec(memory_space=pltpu.VMEM)
    smem = pl.BlockSpec(memory_space=pltpu.SMEM)
    anywhere = pl.BlockSpec(memory_space=pl.ANY)
    unit = (8, ROWS, 128)
    stat = (16, 128)
    dma = pltpu.SemaphoreType.DMA
    n1, n2 = len(STAGE1), len(STAGE2)
    sends = sum(len(onward(key)) for key in ARRIVALS)
    attended, small = pl.pallas_call(
        kernel,
        out_shape=(
            jax.ShapeDtypeStruct((2, SPAN, 2 * WIDE), BF16),
            jax.ShapeDtypeStruct((8, 128), F32),
        ),
        in_specs=[anywhere, smem, vmem, smem, anywhere, anywhere, anywhere],
        out_specs=(vmem, vmem),
        scratch_shapes=[
            pltpu.VMEM(queries.shape, BF16),
            pltpu.VMEM(span_key_value.shape, BF16),
            pltpu.VMEM(w_cand.shape, BF16),
            pltpu.VMEM((128, 128), F32),
            pltpu.VMEM((128, SPAN, WIDE), BF16),
            pltpu.VMEM((128, SPAN, WIDE), BF16),
            pltpu.VMEM(key_value_cache.shape, BF16),
            pltpu.VMEM((SLOTS, 2, ROWS, 128), F32),
            pltpu.VMEM((SLOTS + 3, 2, ROWS, 128), F32),
            pltpu.VMEM((2, 16, 8, 128), F32),
            pltpu.VMEM((2, 16, 8, 128), F32),
            pltpu.VMEM((2, 8, 128), F32),
            pltpu.VMEM((128, 128), F32),
            pltpu.VMEM((16, *unit), BF16),
            pltpu.VMEM((16, *stat), F32),
            pltpu.VMEM((16, *unit), BF16),
            pltpu.VMEM((16, *stat), F32),
            pltpu.VMEM((n1, *unit), BF16),
            pltpu.VMEM((n1, *stat), F32),
            pltpu.VMEM((n1, *unit), BF16),
            pltpu.VMEM((n1, *stat), F32),
            pltpu.VMEM((n2, 2, ROWS, 128), BF16),
            pltpu.VMEM((n2, 8, 128), F32),
            pltpu.VMEM((n2, 2, ROWS, 128), BF16),
            pltpu.VMEM((n2, 8, 128), F32),
            pltpu.VMEM((8, ROWS, 128), F32),
            pltpu.VMEM((4, 8, 128), F32),
            pltpu.VMEM((16, ROWS, 128), F32),
            pltpu.VMEM((8, 8, 128), F32),
            pltpu.VMEM((NY, 2 * SPAN, NCAND), F32),
            pltpu.VMEM((2 * NX, 8, 128), F32),
            pltpu.VMEM((NZ, 8, 128), F32),
            dma((4,)),
            dma((sends,)), dma((len(ARRIVALS),)), dma((NZ + NX,)), dma((NZ + NX,)),
            dma((32,)), dma((32,)), dma((n1, 2)), dma((n1, 2)), dma((n2, 2)), dma((n2, 2)),
            dma((17,)), dma((17,)),
        ],
        compiler_params=pltpu.CompilerParams(
            collective_id=0, has_side_effects=True, vmem_limit_bytes=60 * 1024 * 1024
        ),
        name="score_chains",
    )(queries, idx, idx, answer_id, key_value_cache, span_key_value, w_cand)
    attended, score, tally = pl.pallas_call(
        hand_out,
        out_shape=(
            jax.ShapeDtypeStruct(attended.shape, BF16),
            jax.ShapeDtypeStruct((2,), F32),
            jax.ShapeDtypeStruct((2, 8), F32),
        ),
        in_specs=[vmem, vmem],
        out_specs=(vmem, smem, vmem),
        name="hand_out",
    )(attended, small)
    return attended, score, tally.T


def solution(mesh):
    in_specs = (
        P("dp", None, "mp"),
        P("dp", None, None, "mp"),
        P("dp"),
        P("dp", None, None, "mp"),
        P("dp"),
        P("mp", None),
    )
    out_specs = (P("dp", None, "mp"), P("dp"), P(None, "dp"))
    return jax.shard_map(
        per_device, mesh=mesh, in_specs=in_specs, out_specs=out_specs, check_vma=False
    )
```

time: 102 us -> 93.5 us (0.917)
  Pallas kernels: 95.5 us -> 90.5 us
  local copies, waits for them, and re-layouts: 4.57 us -> 0 us
  other arithmetic: 1 us -> 2.05 us
    pallas_call x1, Pallas kernels: 95.5 us -> 89 us  [per_device(): pl.pallas_call(kernel, out_shape=(jax.ShapeDtypeStruct((2, SPAN, 2 * WIDE...]
    unnamed x2 -> x0, local copies, waits for them, and re-layouts: 2.63 us -> none
    pallas_call x0 -> x1, Pallas kernels: none -> 1.54 us  [per_device(): pl.pallas_call(hand_out, out_shape=(jax.ShapeDtypeStruct(attended.shape,...]
    pallas_call x1 -> x0, local copies, waits for them, and re-layouts: 1.32 us -> none  [per_device(): pl.pallas_call(kernel, out_shape=(jax.ShapeDtypeStruct((2, SPAN, 2 * WIDE...]
    reduce_max x1, other arithmetic: 0.27 us -> 1.29 us  [tables(): return jnp.max(jnp.where(hit, value, jnp.where(first, 0, -1)), axis=2)]
where the time goes in v2:
time: 93.5 us; the launch traced here: 93.3 us
  Pallas kernels  90.5 us (97%)
  other arithmetic  2.05 us (2%)
    pallas_call x1, Pallas kernels, per_device(): pl.pallas_call(kernel, out_shape=(jax.ShapeDtypeStruct((2, SPAN, 2 * WIDE...  89 us

profile of v2, /device:TPU:1, one launch (start us, length us, event | category | flops | bytes accessed | tf_op | source)
XLA Modules:
  0.0 93.3 jit_solution(15626466640563200278)
XLA Ops:
  0.8 0.7 multiply_add_fusion.1
  1.5 1.3 %select_reduce_fusion.idx_s.idx_v = s32[8,128]{1,0:T(8,128)} fusion(s32[8]{0:T(128)S(1)} %broadcast_select_fusion, s32[128]{0:T(128)S(1)} %get-tuple-element.32, s32[128]{0:T(128)S(1)} %get-tuple-element.13, s32[128]{0:T(128)S(1)} %get-tuple-element.35, s32[128]{0:T(128)S(1)} %get-tuple-element.18, s32[128]{0:T(128)S(1)} %get-tuple-element.31, ...), kind=kLoop, calls=%fused_computation.36 | loop fusion | flops 9436160 | bytes 12112 | tf_op jit(solution)/shard_map/reduce_max | solution.py:524
  2.8 89.0 %score_chains.1 = (bf16[2,16,1280]{2,1,0:T(8,128)(2,1)}, f32[8,128]{1,0:T(8,128)}) custom-call(bf16[2,16,1280]{2,1,0:T(8,128)(2,1)} %q_hbm.1, s32[8,128]{1,0:T(8,128)} %select_reduce_fusion.idx_s.idx_v, s32[8,128]{1,0:T(8,128)} %select_reduce_fusion.idx_s.idx_v, s32[2]{0:T(128)} %ans_s.1, bf16[48,2,128,256]{3,2,1,0:T(8,128)(2,1)} %kv_hbm.1, ...), custom_call_target="tpu_custom_call" | custom-call | tf_op jit(solution)/shard_map/score_chains/pallas_call | solution.py:537
  91.7 1.5 %hand_out.1 = (bf16[2,16,1280]{2,1,0:T(8,128)(2,1)}, f32[2]{0:T(128)}, f32[2,8]{1,0:T(2,128)}) custom-call(bf16[2,16,1280]{2,1,0:T(8,128)(2,1)} %get-tuple-element.8.att_ref, f32[8,128]{1,0:T(8,128)} %get-tuple-element.9.small_ref), custom_call_target="tpu_custom_call" | custom-call | tf_op jit(solution)/shard_map/hand_out/pallas_call | solution.py:588
  (13 shorter events, 0.1 us)

commit v3 on v2

--- a/solution.py
+++ b/solution.py
@@ -16,6 +16,7 @@
 EMPTY = SLOTS
 OWN = SLOTS + 1
 NX, NZ, NY = 4, 8, 4
+UNROLL = 8
 big_neg = -1e30
 SCALE = HEAD_SIZE ** (-0.5)
 F32 = jnp.float32
@@ -64,7 +65,7 @@
 
 
 STAGE1 = [(0, arm, k, half) for arm, top in (("L", 4), ("S", 3)) for k in range(1, top + 1) for half in (0, 1)]
-STAGE1 += [(1, arm, k, half) for arm, top in (("L", 2), ("S", 1)) for k in range(1, top + 1) for half in (0, 1)]
+STAGE1 += [(1, arm, k, part) for arm, top in (("L", 2), ("S", 1)) for k in range(1, top + 1) for part in range(4)]
 STAGE2 = {
     (0, "L", 2): ("x++", None), (0, "L", 1): ("x+", None), (0, "S", 1): ("x-", None),
     (1, "L", 4): ("z++", None), (1, "L", 3): ("z++", None),
@@ -76,15 +77,17 @@
 MSG2 = {key: i for i, key in enumerate(STAGE2)}
 STEPS = [
     ("sb", 0, 4, 0), ("sb", 1, 2, 0), ("sb", 1, 2, 1), ("sb", 0, -3, 0),
-    ("sb", 0, 3, 0), ("sb", 0, -2, 0), ("r1", 0, "L", 4, 0), ("r1", 0, "L", 4, 1),
-    ("r1", 1, "L", 2, 0), ("r1", 1, "L", 2, 1), ("sb", 0, 2, 0), ("r1", 0, "S", 3, 0),
-    ("r1", 0, "S", 3, 1), ("sb", 1, -1, 0), ("sb", 1, -1, 1), ("sb", 1, 1, 0),
-    ("sb", 1, 1, 1), ("sb", 0, -1, 0), ("sb", 0, 1, 0), ("sb", 0, 0, 0),
-    ("sb", 1, 0, 0), ("sb", 1, 0, 1), ("r1", 1, "S", 1, 0), ("r1", 1, "S", 1, 1),
-    ("r1", 0, "L", 3, 0), ("r1", 0, "S", 2, 0), ("r1", 0, "L", 3, 1), ("r1", 1, "L", 1, 0),
-    ("r1", 0, "S", 2, 1), ("r1", 0, "L", 2, 0), ("r1", 0, "S", 1, 0), ("r1", 1, "L", 1, 1),
-    ("r1", 0, "L", 2, 1), ("r1", 0, "S", 1, 1), ("r1", 0, "L", 1, 0), ("h1", 1, 0),
-    ("r1", 0, "L", 1, 1), ("h1", 1, 1), ("r2", 1, "L", 4), ("r2", 1, "L", 3),
+    ("sb", 0, 3, 0), ("sb", 0, -2, 0), ("sb", 0, 2, 0), ("sb", 1, -1, 0),
+    ("sb", 1, -1, 1), ("sb", 1, 1, 0), ("sb", 1, 1, 1), ("r1", 0, "L", 4, 0),
+    ("r1", 0, "L", 4, 1), ("r1", 1, "L", 2, 0), ("r1", 1, "L", 2, 1), ("r1", 1, "L", 2, 2),
+    ("r1", 1, "L", 2, 3), ("sb", 0, -1, 0), ("r1", 0, "S", 3, 0), ("r1", 0, "S", 3, 1),
+    ("sb", 0, 1, 0), ("sb", 0, 0, 0), ("sb", 1, 0, 0), ("sb", 1, 0, 1),
+    ("r1", 1, "S", 1, 0), ("r1", 1, "S", 1, 1), ("r1", 1, "S", 1, 2), ("r1", 1, "S", 1, 3),
+    ("r1", 0, "L", 3, 0), ("r1", 1, "L", 1, 0), ("r1", 0, "S", 2, 0), ("r1", 0, "L", 3, 1),
+    ("r1", 1, "L", 1, 1), ("r1", 0, "S", 2, 1), ("r1", 1, "L", 1, 2), ("r1", 0, "L", 2, 0),
+    ("r1", 1, "L", 1, 3), ("r1", 0, "S", 1, 0), ("r1", 0, "L", 2, 1), ("h1", 1, 0),
+    ("r1", 0, "S", 1, 1), ("h1", 1, 1), ("r1", 0, "L", 1, 0), ("h1", 1, 2),
+    ("r1", 0, "L", 1, 1), ("h1", 1, 3), ("r2", 1, "L", 4), ("r2", 1, "L", 3),
     ("r2", 1, "S", 3), ("r2", 1, "S", 2), ("h1", 0, 0), ("h1", 0, 1),
     ("r2", 0, "L", 2), ("r2", 0, "L", 1), ("r2", 0, "S", 1), ("r2", 1, "L", 2),
     ("r2", 1, "S", 1), ("r2", 1, "L", 1), ("h2", 0), ("h2", 1),
@@ -92,9 +95,9 @@
 
 
 def kernel(
-    q_hbm, idx_s, idx_v, ans_s, kv_hbm, span_hbm, w_hbm,
+    q_hbm, tags_ref, ans_s, kv_hbm, span_hbm, w_hbm,
     att_ref, small_ref,
-    q_ref, span_ref, w_ref, ring_tally,
+    q_ref, span_ref, w_ref, ring_tally, tags_v, idx_v, idx_s,
     g0, g1, kv, sbuf, res, dm, dl, spst, fscr,
     sib_s, sib_ss, sib_r, sib_rs, m1_s, m1_ss, m1_r, m1_rs, m2_s, m2_ss, m2_r, m2_rs,
     r0, r0s, r1, r1s, lg, ta, tz,
@@ -177,6 +180,35 @@
 
     def as_rows(mat):
         return jnp.concatenate([mat, jnp.zeros((128 - ROWS, 128), F32)], axis=0).T
+
+    square = lax.broadcasted_iota(jnp.int32, (128, 128), 0)
+
+    def tables():
+        tags_v[...] = jnp.full((8, 128), -1, jnp.int32)
+        for i in range(8):
+            tags_v[i : i + 1, 0:SLOTS] = tags_ref[...]
+        tag = tags_v[0:1, :]
+        down = jnp.concatenate([tags_v[...]] * 16, axis=0).T
+        e = lax.broadcasted_iota(jnp.int32, (1, 128), 1)
+        b = square
+        c, ecore = e % 2, e // 64
+        tc, tcore, tz_, tx_ = tag % 2, (tag // 2) % 2, (tag // 4) % NZ, tag // (4 * NZ)
+        idx_v[0:1, :] = ((tcore * NZ + tz_) * NX + tx_) * 2 + tc
+        idx_v[1:2, :] = ((tcore * NX + tx_) * NZ + tz_) * 2 + tc
+        chains = (
+            ((((e // 2) % NX) * NZ + (e // 8) % NZ) * 2 + ecore) * 2 + c,
+            ((((e // 16) % NX) * NZ + (e // 2) % NZ) * 2 + ecore) * 2 + c,
+        )
+        for h in range(2):
+            hit = down == chains[h]
+            idx_v[2 + 2 * h : 3 + 2 * h, :] = jnp.max(jnp.where(hit, EMPTY - b, 0), axis=0, keepdims=True)
+            idx_v[3 + 2 * h : 4 + 2 * h, :] = jnp.max(jnp.where(hit, b, -1), axis=0, keepdims=True)
+        twin = (down == tag) & (b != e) & (b < SLOTS)
+        idx_v[6:7, :] = jnp.max(jnp.where(twin, b, -1), axis=0, keepdims=True)
+        idx_v[7:8, :] = e
+        copy = pltpu.make_async_copy(idx_v, idx_s, in_sem.at[4])
+        copy.start()
+        return copy
 
     def own_spans():
         span_copy.wait()
@@ -202,6 +234,8 @@
     for step, key in enumerate(ARRIVALS):
         if step == 2:
             kv_copy.start()
+        if step == 8:
+            tables_copy = tables()
         if step == 12:
             own_spans()
         head, xr, zr = key
@@ -229,37 +263,33 @@
             xx = along_x(xr)
             rows = g1.at[pl.ds((core * NX + xx) * NZ * 2, NZ * 2)]
             send(rows, rows, sg_send.at[NZ + xx], sg_recv.at[NZ + xx], sibling)
+    tables_copy.wait()
+    kv_copy.wait()
+
+    def scores_of(h):
+        def score_step(i, top):
+            for u in range(UNROLL):
+                b = i * UNROLL + u
+                q = query_rows(gathered[h][idx_s[h, b]])
+                k = kv[b, 0, :, h * 128 : (h + 1) * 128]
+                sc = lax.dot_general(q, k, (((1,), (1,)), ((), ())), preferred_element_type=F32) * SCALE
+                sbuf[b, h] = sc
+                top = jnp.where(lanes == b, jnp.max(sc, axis=1, keepdims=True), top)
+            return top
+
+        return lax.fori_loop(0, SLOTS // UNROLL, score_step, jnp.full((ROWS, 128), big_neg, F32))
+
+    for xx in range(NX):
+        rows = g1.at[pl.ds((other * NX + xx) * NZ * 2, NZ * 2)]
+        arrived(rows, sg_send.at[NZ + xx], sg_recv.at[NZ + xx])
+    top1 = scores_of(1)
     for zz in range(NZ):
         rows = g0.at[pl.ds((other * NZ + zz) * NX * 2, NX * 2)]
         arrived(rows, sg_send.at[zz], sg_recv.at[zz])
-    for xx in range(NX):
-        rows = g1.at[pl.ds((other * NX + xx) * NZ * 2, NZ * 2)]
-        arrived(rows, sg_send.at[NZ + xx], sg_recv.at[NZ + xx])
-    kv_copy.wait()
-
-    def score_block(b, carry):
-        out = []
-        for h in range(2):
-            q = query_rows(gathered[h][idx_s[h, b]])
-            k = kv[b, 0, :, h * 128 : (h + 1) * 128]
-            sc = lax.dot_general(q, k, (((1,), (1,)), ((), ())), preferred_element_type=F32) * SCALE
-            sbuf[b, h] = sc
-            out.append(jnp.where(lanes == b, jnp.max(sc, axis=1, keepdims=True), carry[h]))
-        return tuple(out)
-
-    UNROLL = 4
-
-    def score_step(i, carry):
-        for u in range(UNROLL):
-            carry = score_block(i * UNROLL + u, carry)
-        return carry
-
-    tops = lax.fori_loop(0, SLOTS // UNROLL, score_step, (jnp.full((ROWS, 128), big_neg, F32),) * 2)
-
-    square = lax.broadcasted_iota(jnp.int32, (128, 128), 0)
-
-    def pick(mat, wanted):
-        hot = (square == wanted).astype(F32)
+    tops = (scores_of(0), top1)
+
+    def pick(mat, *wanted):
+        hot = sum((square == w).astype(F32) for w in wanted)
         return jnp.dot(mat, hot, precision=lax.Precision.HIGHEST, preferred_element_type=F32)
 
     twin = idx_v[6:7, :]
@@ -277,11 +307,11 @@
         return tuple(out)
 
     def weigh_step(i, carry):
-        for u in range(UNROLL):
-            carry = weigh_block(i * UNROLL + u, carry)
+        for u in range(UNROLL // 2):
+            carry = weigh_block(i * (UNROLL // 2) + u, carry)
         return carry
 
-    sums = lax.fori_loop(0, SLOTS // UNROLL, weigh_step, (jnp.zeros((ROWS, 128), F32),) * 2)
+    sums = lax.fori_loop(0, 2 * SLOTS // UNROLL, weigh_step, (jnp.zeros((ROWS, 128), F32),) * 2)
 
     for h in range(2):
         res[EMPTY, h] = jnp.zeros((ROWS, 128), F32)
@@ -289,7 +319,7 @@
         last = idx_v[3 + 2 * h : 4 + 2 * h, :]
         last = jnp.where(last > first, last, EMPTY)
         dm[h] = as_rows(pick(tops[h], first)).reshape(16, 8, 128)
-        dl[h] = as_rows(pick(sums[h], first) + pick(sums[h], last)).reshape(16, 8, 128)
+        dl[h] = as_rows(pick(sums[h], first, last)).reshape(16, 8, 128)
 
     def merge(n, sources, emit, normal=False):
         top = sources[0][1]
@@ -365,10 +395,10 @@
         return (lambda j: m2_r[at, j].astype(F32)), m2_rs[at, 0:2, :], m2_rs[at, 2:4, :]
 
     def local(h, k, half):
-        g = group_at(h, k, half)
-        first, n = (half * 4, 4) if h == 0 else (0, 8)
-        key = (h, k) if h == 0 else (h, k, half)
-        return n, [held(h, core, g, first, n), from_sibling(h, g, key, first, n)]
+        block = 0 if h == 0 else half // 2
+        g = group_at(h, k, block)
+        first, n = (half % 2) * 4, 4
+        return n, [held(h, core, g, first, n), from_sibling(h, g, (h, k, block), first, n)]
 
     def ring1(h, arm, k, half):
         at = MSG1[(h, arm, k, half)]
@@ -507,25 +537,7 @@
     score_ref[1] = small_ref[3, 0]
 
 
-def tables(tags):
-    r, e, b = (lax.broadcasted_iota(jnp.int32, (8, 128, 128), axis) for axis in range(3))
-    c, core = e % 2, e // 64
-    chain0 = ((((e // 2) % NX) * NZ + (e // 8) % NZ) * 2 + core) * 2 + c
-    chain1 = ((((e // 16) % NX) * NZ + (e // 2) % NZ) * 2 + core) * 2 + c
-    padded = jnp.pad(tags, (0, 128 - SLOTS), constant_values=-1)
-    tag, mine = padded[None, None, :], padded[None, :, None]
-    tc, tcore, tz, tx = tag % 2, (tag // 2) % 2, (tag // 4) % NZ, tag // (4 * NZ)
-    place0 = ((tcore * NZ + tz) * NX + tx) * 2 + tc
-    place1 = ((tcore * NX + tx) * NZ + tz) * 2 + tc
-    wanted = jnp.where(r < 4, chain0, jnp.where(r < 6, chain1, mine))
-    hit = jnp.where(r < 2, b == e, (tag == wanted) & ((r < 6) | (b != e))) & (b < SLOTS)
-    first = (r == 2) | (r == 4)
-    value = jnp.where(first, EMPTY - b, jnp.where(r == 0, place0, jnp.where(r == 1, place1, b)))
-    return jnp.max(jnp.where(hit, value, jnp.where(first, 0, -1)), axis=2)
-
-
 def per_device(queries, key_value_cache, slot_tags, span_key_value, answer_id, w_cand):
-    idx = tables(slot_tags)
     vmem = pl.BlockSpec(memory_space=pltpu.VMEM)
     smem = pl.BlockSpec(memory_space=pltpu.SMEM)
     anywhere = pl.BlockSpec(memory_space=pl.ANY)
@@ -540,13 +552,16 @@
             jax.ShapeDtypeStruct((2, SPAN, 2 * WIDE), BF16),
             jax.ShapeDtypeStruct((8, 128), F32),
         ),
-        in_specs=[anywhere, smem, vmem, smem, anywhere, anywhere, anywhere],
+        in_specs=[anywhere, vmem, smem, anywhere, anywhere, anywhere],
         out_specs=(vmem, vmem),
         scratch_shapes=[
             pltpu.VMEM(queries.shape, BF16),
             pltpu.VMEM(span_key_value.shape, BF16),
             pltpu.VMEM(w_cand.shape, BF16),
             pltpu.VMEM((128, 128), F32),
+            pltpu.VMEM((8, 128), jnp.int32),
+            pltpu.VMEM((8, 128), jnp.int32),
+            pltpu.SMEM((8, 128), jnp.int32),
             pltpu.VMEM((128, SPAN, WIDE), BF16),
             pltpu.VMEM((128, SPAN, WIDE), BF16),
             pltpu.VMEM(key_value_cache.shape, BF16),
@@ -560,10 +575,10 @@
             pltpu.VMEM((16, *stat), F32),
             pltpu.VMEM((16, *unit), BF16),
             pltpu.VMEM((16, *stat), F32),
-            pltpu.VMEM((n1, *unit), BF16),
-            pltpu.VMEM((n1, *stat), F32),
-            pltpu.VMEM((n1, *unit), BF16),
-            pltpu.VMEM((n1, *stat), F32),
+            pltpu.VMEM((n1, 4, ROWS, 128), BF16),
+            pltpu.VMEM((n1, 8, 128), F32),
+            pltpu.VMEM((n1, 4, ROWS, 128), BF16),
+            pltpu.VMEM((n1, 8, 128), F32),
             pltpu.VMEM((n2, 2, ROWS, 128), BF16),
             pltpu.VMEM((n2, 8, 128), F32),
             pltpu.VMEM((n2, 2, ROWS, 128), BF16),
@@ -575,7 +590,7 @@
             pltpu.VMEM((NY, 2 * SPAN, NCAND), F32),
             pltpu.VMEM((2 * NX, 8, 128), F32),
             pltpu.VMEM((NZ, 8, 128), F32),
-            dma((4,)),
+            dma((5,)),
             dma((sends,)), dma((len(ARRIVALS),)), dma((NZ + NX,)), dma((NZ + NX,)),
             dma((32,)), dma((32,)), dma((n1, 2)), dma((n1, 2)), dma((n2, 2)), dma((n2, 2)),
             dma((17,)), dma((17,)),
@@ -584,7 +599,7 @@
             collective_id=0, has_side_effects=True, vmem_limit_bytes=60 * 1024 * 1024
         ),
         name="score_chains",
-    )(queries, idx, idx, answer_id, key_value_cache, span_key_value, w_cand)
+    )(queries, slot_tags[None], answer_id, key_value_cache, span_key_value, w_cand)
     attended, score, tally = pl.pallas_call(
         hand_out,
         out_shape=(

time: 93.5 us -> 89.9 us (0.961)
  other arithmetic: 2.05 us -> 0 us
  Pallas kernels: 90.5 us -> 89.3 us
    reduce_max x1 -> x0, other arithmetic: 1.29 us -> none  [tables(): return jnp.max(jnp.where(hit, value, jnp.where(first, 0, -1)), axis=2)]
    pallas_call x1, Pallas kernels: 89 us -> 87.7 us  [per_device(): pl.pallas_call(kernel, out_shape=(jax.ShapeDtypeStruct((2, SPAN, 2 * WIDE...]
where the time goes in v3:
time: 89.9 us
  Pallas kernels  89.3 us (99%)
    pallas_call x1, Pallas kernels, per_device(): pl.pallas_call(kernel, out_shape=(jax.ShapeDtypeStruct((2, SPAN, 2 * WIDE...  87.7 us

profile of v3, /device:TPU:1, one launch (start us, length us, event | category | flops | bytes accessed | tf_op | source)
XLA Modules:
  0.0 89.9 jit_solution(130337437890899083)
XLA Ops:
  0.6 87.7 %score_chains.1 = (bf16[2,16,1280]{2,1,0:T(8,128)(2,1)}, f32[8,128]{1,0:T(8,128)}) custom-call(bf16[2,16,1280]{2,1,0:T(8,128)(2,1)} %q_hbm.1, s32[1,48]{1,0:T(1,128)} %bitcast.2, s32[2]{0:T(128)} %ans_s.1, bf16[48,2,128,256]{3,2,1,0:T(8,128)(2,1)} %kv_hbm.1, bf16[2,2,16,256]{3,2,1,0:T(8,128)(2,1)} %span_hbm.1, bf16[1280,128]{1,0:T(8,128)(2,1)} %w_hbm.1), custom_call_target="tpu_custom_call" | custom-call | tf_op jit(solution)/shard_map/score_chains/pallas_call | solution.py:549
  88.4 1.5 %hand_out.1 = (bf16[2,16,1280]{2,1,0:T(8,128)(2,1)}, f32[2]{0:T(128)}, f32[2,8]{1,0:T(2,128)}) custom-call(bf16[2,16,1280]{2,1,0:T(8,128)(2,1)} %get-tuple-element.8.att_ref, f32[8,128]{1,0:T(8,128)} %get-tuple-element.9.small_ref), custom_call_target="tpu_custom_call" | custom-call | tf_op jit(solution)/shard_map/hand_out/pallas_call | solution.py:603
